TPU v7x, 32 devices: a 4x4x1 block of a 4x4x8 slice. The times are simulated.
32 devices in a mesh: dp: 1 (over z), tp: 4 (over y), sp: 8 (over x, core).
Axes of the slice: x: 4, y: 4, z: 1, core: 2. Of those that a mesh axis runs over, the one named last changes fastest.
The devices are a block of a 4x4x8 slice.
Arguments:
- x_seq: bfloat16 [6144, 4096], P(('dp', 'sp', 'tp'))
- w_query: bfloat16 [4096, 32, 128], P(None, 'tp')
- w_key: bfloat16 [4096, 8, 128], P(None, 'tp')
- w_value: bfloat16 [4096, 8, 128], P(None, 'tp')
- w_out: bfloat16 [32, 128, 4096], P('tp')
Outputs:
- output: bfloat16 [6144, 4096], P(('dp', 'sp', 'tp'))
All inputs are finite; a program needn't handle non-finite values.
Results may differ from a plain program's by a relative error of at most 0.00855549.
Values are sent between devices in bfloat16 or wider.
A program may use at most 768 MiB of HBM per device.

v0:
```python
import jax
import jax.numpy as jnp
from jax import lax
from jax.sharding import PartitionSpec as P

WINDOW = 4096
NEG_BIG = -1e30


def block_update(soft_state, q_blk, k_blk, v_blk, chunk_gap, score_scale):
    row_max, row_sum, acc_sum = soft_state
    chunk_len = q_blk.shape[0]
    scores = jnp.einsum("qhgd,khd->hgqk", q_blk, k_blk, preferred_element_type=jnp.float32) * score_scale
    offset = chunk_gap * chunk_len + lax.broadcasted_iota(jnp.int32, (chunk_len, chunk_len), 0) - lax.broadcasted_iota(jnp.int32, (chunk_len, chunk_len), 1)
    visible = (offset >= 0) & (offset < WINDOW)
    scores = jnp.where(visible, scores, NEG_BIG)
    new_max = jnp.maximum(row_max, jnp.max(scores, axis=-1))
    prob_blk = jnp.where(visible, jnp.exp(scores - new_max[..., None]), 0.0)
    rescale = jnp.exp(row_max - new_max)
    new_sum = row_sum * rescale + jnp.sum(prob_blk, axis=-1)
    new_acc = acc_sum * rescale[..., None] + jnp.einsum("hgqk,khd->hgqd", prob_blk.astype(jnp.bfloat16), v_blk, preferred_element_type=jnp.float32)
    return new_max, new_sum, new_acc


def pair_update(soft_state, q_blk, k_blk, v_blk, q_id, k_id, score_scale):
    chunk_len = q_blk.shape[0]
    chunk_gap = q_id - k_id
    needed = (chunk_gap >= 0) & (chunk_gap * chunk_len - chunk_len + 1 < WINDOW)
    return lax.cond(needed, lambda cur_state: block_update(cur_state, q_blk, k_blk, v_blk, chunk_gap, score_scale), lambda cur_state: cur_state, soft_state)


def solution(mesh):
    sp_size = mesh.shape["sp"]
    next_pairs = [(src_idx, (src_idx + 1) % sp_size) for src_idx in range(sp_size)]

    def local_attn(x_part, w_query, w_key, w_value, w_out):
        x_block = lax.all_gather(x_part, "tp", axis=0, tiled=True)
        block_rows, d_model = x_block.shape
        chunk_len = block_rows // 2
        heads_loc, head_dim = w_query.shape[1], w_query.shape[2]
        kv_loc = w_key.shape[1]
        group_size = heads_loc // kv_loc
        score_scale = head_dim ** -0.5
        q_loc = jnp.dot(x_block, w_query.reshape(d_model, heads_loc * head_dim), preferred_element_type=jnp.float32).astype(jnp.bfloat16).reshape(2, chunk_len, kv_loc, group_size, head_dim)
        k_loc = jnp.dot(x_block, w_key.reshape(d_model, kv_loc * head_dim), preferred_element_type=jnp.float32).astype(jnp.bfloat16).reshape(2, chunk_len, kv_loc, head_dim)
        v_loc = jnp.dot(x_block, w_value.reshape(d_model, kv_loc * head_dim), preferred_element_type=jnp.float32).astype(jnp.bfloat16).reshape(2, chunk_len, kv_loc, head_dim)
        sp_rank = lax.axis_index("sp")
        own_ids = (sp_rank, 2 * sp_size - 1 - sp_rank)

        def fresh_state():
            return (jnp.full((kv_loc, group_size, chunk_len), NEG_BIG, jnp.float32), jnp.zeros((kv_loc, group_size, chunk_len), jnp.float32), jnp.zeros((kv_loc, group_size, chunk_len, head_dim), jnp.float32))

        def absorb(states, k_blocks, v_blocks, src_rank):
            key_ids = (src_rank, 2 * sp_size - 1 - src_rank)
            updated = []
            for q_half in range(2):
                cur_state = states[q_half]
                for k_half in range(2):
                    cur_state = pair_update(cur_state, q_loc[q_half], k_blocks[k_half], v_blocks[k_half], own_ids[q_half], key_ids[k_half], score_scale)
                updated.append(cur_state)
            return tuple(updated)

        states = absorb((fresh_state(), fresh_state()), k_loc, v_loc, sp_rank)

        def ring_free_step(step_idx, carry):
            k_blocks, v_blocks, cur_states = carry
            k_blocks, v_blocks = lax.ppermute((k_blocks, v_blocks), "sp", next_pairs)
            src_rank = (sp_rank - step_idx) % sp_size
            return k_blocks, v_blocks, absorb(cur_states, k_blocks, v_blocks, src_rank)

        carry_out = lax.fori_loop(1, sp_size, ring_free_step, (k_loc, v_loc, states))
        states = carry_out[2]
        outs_norm = jnp.stack([(soft_state[2] / soft_state[1][..., None]).astype(jnp.bfloat16) for soft_state in states])
        part_sum = jnp.einsum("ahgqd,hgde->aqe", outs_norm, w_out.reshape(kv_loc, group_size, head_dim, d_model), preferred_element_type=jnp.float32).reshape(block_rows, d_model)
        y_rows = lax.psum_scatter(part_sum, "tp", scatter_dimension=0, tiled=True)
        return y_rows.astype(jnp.bfloat16)

    return jax.shard_map(local_attn, mesh=mesh, in_specs=(P(("dp", "sp", "tp"), None), P(None, "tp", None), P(None, "tp", None), P(None, "tp", None), P("tp", None, None)), out_specs=P(("dp", "sp", "tp"), None), check_vma=False)
```

profile of v0, /device:TPU:97, one launch (start us, length us, event | category | flops | bytes accessed | tf_op | source)
XLA Modules:
  0.0 480.8 jit_solution(3867821409604756816)
XLA Ops:
  7.5 68.4 %all-gather.2.cloned.1.call-done = bf16[768,4096]{1,0:T(8,128)(2,1)} async-done(((bf16[192,4096]{1,0:T(8,128)(2,1)}), bf16[768,4096]{1,0:T(8,128)(2,1)}) %all-gather.2.cloned.1.call-update) | async-done | bytes 6291472 | tf_op jit(solution)/shard_map/all_gather | solution.py:37
  75.8 11.2 %fusion.132 = bf16[768,1024]{1,0:T(8,128)(2,1)S(1)} fusion(bf16[768,4096]{1,0:T(8,128)(2,1)} %all-gather.2.cloned.1.call-done, bf16[512,8,8,128]{3,2,1,0:T(8,128)(2,1)} %bitcast.325), kind=kOutput, calls=%fused_computation.161 | convolution fusion | flops 6443237376 | bytes 16252928 | tf_op jit(solution)/shard_map/dot_general | solution.py:44
  88.0 2.3 reshape.68
  90.3 5.2 %fusion.140 = bf16[768,256]{0,1:T(8,128)(2,1)S(1)} fusion(bf16[768,4096]{1,0:T(8,128)(2,1)} %all-gather.2.cloned.1.call-done, bf16[512,8,2,128]{3,2,1,0:T(2,128)(2,1)} %bitcast.327), kind=kOutput, calls=%fused_computation.167 | convolution fusion | flops 1610809344 | bytes 8781824 | tf_op jit(solution)/shard_map/dot_general | solution.py:45
  96.5 5.3 %fusion.143 = bf16[768,256]{0,1:T(8,128)(2,1)S(1)} fusion(bf16[768,4096]{1,0:T(8,128)(2,1)} %all-gather.2.cloned.1.call-done, bf16[512,8,2,128]{3,2,1,0:T(2,128)(2,1)} %bitcast.328), kind=kOutput, calls=%fused_computation.168 | convolution fusion | flops 1610809344 | bytes 8781824 | tf_op jit(solution)/shard_map/dot_general | solution.py:46
  105.4 3.8 fusion.115
  116.0 5.1 %fusion.119 = (f32[2,4,384]{2,1,0:T(4,128)S(1)}, f32[2,4,384]{2,1,0:T(4,128)S(1)}) fusion(f32[2,384,384,4]{2,1,3,0:T(8,128)} %get-tuple-element.762, f32[2,4,384]{2,1,0:T(4,128)S(1)} %max.19, pred[384,384]{0,1:T(8,128)(4,1)S(1)} %fusion.154, f32[2,4,384]{2,1,0:T(4,128)S(1)} %broadcast_maximum_fusion.1, f32[2,384,384,4]{2,1,3,0:T(8,128)} %copy-done), kind=kLoop, calls=%fused_computation.150 | loop fusion | flops 11790336 | bytes 9633792 | tf_op jit(solution)/shard_map/cond/branch_1_fun/reduce_sum | solution.py:20
  122.4 5.4 %fusion.135 = f32[2,4,384,128]{3,2,1,0:T(8,128)} fusion(bf16[384,2,128,1]{0,2,3,1:T(8,128)(2,1)S(1)} %bitcast.322, f32[2,384,384,4]{2,1,3,0:T(8,128)} %copy-done, f32[2,4,384]{2,1,0:T(4,128)S(1)} %broadcast_maximum_fusion.1, pred[384,384]{0,1:T(8,128)(4,1)S(1)} %fusion.154, f32[2,4,384]{2,1,0:T(4,128)S(1)} %get-tuple-element.764), kind=kOutput, calls=%fused_computation.166 | convolution fusion | flops 308281344 | bytes 6660096 | tf_op jit(solution)/shard_map/cond/branch_1_fun/hgqk,khd->hgqd/dot_general | solution.py:21
  127.8 4.0 multiply_add_fusion.10
  131.8 198.8 %while.32 = (s32[]{:T(128)}, bf16[2,384,2,128]{3,1,2,0:T(8,128)(2,1)}, bf16[2,384,2,128]{3,1,2,0:T(8,128)(2,1)}, f32[2,4,384]{2,1,0:T(4,128)S(1)}, f32[2,4,384]{...) while((s32[]{:T(128)}, ...), condition=%wide.region_29.30_spmd, body=%wide.region_12.29_spmd.sunk | while | flops 2482791936 | bytes 140293712 | solution.py:71
  131.8 8.1 %collective-permute-start = (bf16[2,384,2,128]{3,1,2,0:T(8,128)(2,1)}, bf16[2,384,2,128]{3,1,2,0:T(8,128)(2,1)}, u32[]{:S(2)}, u32[]{:S(2)}) collective-permute-start(bf16[2,384,2,128]{3,1,2,0:T(8,128)(2,1)} %get-tuple-element.941), channel_id=1, source_target_pairs={{0,1},{1,2},{2,3},{3,4},{4,5},{5,6},{6,7},{7,0},{8,9},{9,10},{10,1... | collective-permute-start | bytes 1179656 | tf_op jit(solution)/shard_map/while/body/eval_jaxpr/ppermute | solution.py:67
  140.1 4.6 collective-permute-done
  145.7 3.2 collective-permute-done.1
  150.7 6.9 %conditional.12 = ((f32[2,4,384]{2,1,0:T(4,128)S(1)}, f32[2,4,384]{2,1,0:T(4,128)}, f32[2,4,384,128]{3,2,1,0:T(8,128)})) conditional(s32[]{:T(128)} %convert_element_type.162, (f32[2,4,384]{2,1,0:T(4,128)S(1)}, f32[2,4,384]{2,1,0:T(4,128)}, f32[2,4,384,128]{3,2,1,0:T(8,128)}) %tuple.140, (s32[]{:T(128)}, bf16[384,2,128]{2,0,1:T(8,128)(2,1)S(1)}, ...), branch_computations={%region_13.13_spmd, %region_14.16_spmd} | conditional | flops 620697984 | bytes 32640132 | solution.py:29
  161.1 2.5 collective-permute-start
  163.6 4.7 collective-permute-start.1
  170.2 2.8 collective-permute-done.1
  174.8 5.6 %conditional.14 = ((f32[2,4,384]{2,1,0:T(4,128)}, f32[2,4,384]{2,1,0:T(4,128)}, f32[2,4,384,128]{3,2,1,0:T(8,128)})) conditional(s32[]{:T(128)} %convert_element_type.164, (f32[2,4,384]{2,1,0:T(4,128)}, f32[2,4,384]{2,1,0:T(4,128)}, f32[2,4,384,128]{3,2,1,0:T(8,128)}) %tuple.143, (s32[]{:T(128)}, bf16[384,2,128]{2,0,1:T(8,128)(2,1)S(1)}, ...), branch_computations={%region_21.21_spmd, %region_22.0_spmd} | conditional | flops 620697984 | bytes 32787672 | solution.py:29
  177.1 2.1 multiply_add_fusion.6
  180.4 5.6 %conditional.15 = ((f32[2,4,384]{2,1,0:T(4,128)}, f32[2,4,384]{2,1,0:T(4,128)}, f32[2,4,384,128]{3,2,1,0:T(8,128)})) conditional(s32[]{:T(128)} %convert_element_type.163, (f32[2,4,384]{2,1,0:T(4,128)}, f32[2,4,384]{2,1,0:T(4,128)}, f32[2,4,384,128]{3,2,1,0:T(8,128)}) %get-tuple-element.983, (s32[]{:T(128)}, bf16[384,2,128]{2,0,1:T(8,128)(2,1)S(1)}, ...), branch_computations={%region_25.25_spmd, %region_26.0_spmd} | conditional | flops 620697984 | bytes 32787672 | solution.py:29
  190.5 7.0 %collective-permute-start.1 = (bf16[2,384,2,128]{3,1,2,0:T(8,128)(2,1)}, bf16[2,384,2,128]{3,1,2,0:T(8,128)(2,1)}, u32[]{:S(2)}, u32[]{:S(2)}) collective-permute-start(bf16[2,384,2,128]{3,1,2,0:T(8,128)(2,1)} %get-tuple-element.942), channel_id=1, source_target_pairs={{0,1},{1,2},{2,3},{3,4},{4,5},{5,6},{6,7},{7,0},{8,9},{9,10},{10,1... | collective-permute-start | bytes 1179656 | tf_op jit(solution)/shard_map/while/body/eval_jaxpr/ppermute | solution.py:67
  204.1 5.6 %conditional.14 = ((f32[2,4,384]{2,1,0:T(4,128)}, f32[2,4,384]{2,1,0:T(4,128)}, f32[2,4,384,128]{3,2,1,0:T(8,128)})) conditional(s32[]{:T(128)} %convert_element_type.164, (f32[2,4,384]{2,1,0:T(4,128)}, f32[2,4,384]{2,1,0:T(4,128)}, f32[2,4,384,128]{3,2,1,0:T(8,128)}) %tuple.143, (s32[]{:T(128)}, bf16[384,2,128]{2,0,1:T(8,128)(2,1)S(1)}, ...), branch_computations={%region_21.21_spmd, %region_22.0_spmd} | conditional | flops 620697984 | bytes 32787672 | solution.py:29
  209.7 5.6 %conditional.15 = ((f32[2,4,384]{2,1,0:T(4,128)}, f32[2,4,384]{2,1,0:T(4,128)}, f32[2,4,384,128]{3,2,1,0:T(8,128)})) conditional(s32[]{:T(128)} %convert_element_type.163, (f32[2,4,384]{2,1,0:T(4,128)}, f32[2,4,384]{2,1,0:T(4,128)}, f32[2,4,384,128]{3,2,1,0:T(8,128)}) %get-tuple-element.983, (s32[]{:T(128)}, bf16[384,2,128]{2,0,1:T(8,128)(2,1)S(1)}, ...), branch_computations={%region_25.25_spmd, %region_26.0_spmd} | conditional | flops 620697984 | bytes 32787672 | solution.py:29
  212.0 2.1 multiply_add_fusion.8
  219.8 2.5 collective-permute-start
  222.4 7.0 %collective-permute-done = bf16[2,384,2,128]{3,1,2,0:T(8,128)(2,1)} collective-permute-done((bf16[2,384,2,128]{3,1,2,0:T(8,128)(2,1)}, bf16[2,384,2,128]{3,1,2,0:T(8,128)(2,1)}, u32[]{:S(2)}, u32[]{:S(2)}) %collective-permute-start) | collective-permute-done | bytes 393248 | tf_op jit(solution)/shard_map/while/body/eval_jaxpr/ppermute | solution.py:67
  233.0 5.6 %conditional.14 = ((f32[2,4,384]{2,1,0:T(4,128)}, f32[2,4,384]{2,1,0:T(4,128)}, f32[2,4,384,128]{3,2,1,0:T(8,128)})) conditional(s32[]{:T(128)} %convert_element_type.164, (f32[2,4,384]{2,1,0:T(4,128)}, f32[2,4,384]{2,1,0:T(4,128)}, f32[2,4,384,128]{3,2,1,0:T(8,128)}) %tuple.143, (s32[]{:T(128)}, bf16[384,2,128]{2,0,1:T(8,128)(2,1)S(1)}, ...), branch_computations={%region_21.21_spmd, %region_22.0_spmd} | conditional | flops 620697984 | bytes 32787672 | solution.py:29
  235.4 2.1 multiply_add_fusion.6
  238.7 5.6 %conditional.15 = ((f32[2,4,384]{2,1,0:T(4,128)}, f32[2,4,384]{2,1,0:T(4,128)}, f32[2,4,384,128]{3,2,1,0:T(8,128)})) conditional(s32[]{:T(128)} %convert_element_type.163, (f32[2,4,384]{2,1,0:T(4,128)}, f32[2,4,384]{2,1,0:T(4,128)}, f32[2,4,384,128]{3,2,1,0:T(8,128)}) %get-tuple-element.983, (s32[]{:T(128)}, bf16[384,2,128]{2,0,1:T(8,128)(2,1)S(1)}, ...), branch_computations={%region_25.25_spmd, %region_26.0_spmd} | conditional | flops 620697984 | bytes 32787672 | solution.py:29
  241.0 2.1 multiply_add_fusion.8
  248.8 2.5 collective-permute-start
  251.3 4.5 collective-permute-start.1
  255.9 3.7 collective-permute-done
  262.5 5.6 %conditional.14 = ((f32[2,4,384]{2,1,0:T(4,128)}, f32[2,4,384]{2,1,0:T(4,128)}, f32[2,4,384,128]{3,2,1,0:T(8,128)})) conditional(s32[]{:T(128)} %convert_element_type.164, (f32[2,4,384]{2,1,0:T(4,128)}, f32[2,4,384]{2,1,0:T(4,128)}, f32[2,4,384,128]{3,2,1,0:T(8,128)}) %tuple.143, (s32[]{:T(128)}, bf16[384,2,128]{2,0,1:T(8,128)(2,1)S(1)}, ...), branch_computations={%region_21.21_spmd, %region_22.0_spmd} | conditional | flops 620697984 | bytes 32787672 | solution.py:29
  268.2 5.6 %conditional.15 = ((f32[2,4,384]{2,1,0:T(4,128)}, f32[2,4,384]{2,1,0:T(4,128)}, f32[2,4,384,128]{3,2,1,0:T(8,128)})) conditional(s32[]{:T(128)} %convert_element_type.163, (f32[2,4,384]{2,1,0:T(4,128)}, f32[2,4,384]{2,1,0:T(4,128)}, f32[2,4,384,128]{3,2,1,0:T(8,128)}) %get-tuple-element.983, (s32[]{:T(128)}, bf16[384,2,128]{2,0,1:T(8,128)(2,1)S(1)}, ...), branch_computations={%region_25.25_spmd, %region_26.0_spmd} | conditional | flops 620697984 | bytes 32787672 | solution.py:29
  270.5 2.1 multiply_add_fusion.8
  278.3 2.3 collective-permute-start
  280.6 4.5 collective-permute-start.1
  286.3 3.5 collective-permute-done.1
  291.6 5.6 %conditional.14 = ((f32[2,4,384]{2,1,0:T(4,128)}, f32[2,4,384]{2,1,0:T(4,128)}, f32[2,4,384,128]{3,2,1,0:T(8,128)})) conditional(s32[]{:T(128)} %convert_element_type.164, (f32[2,4,384]{2,1,0:T(4,128)}, f32[2,4,384]{2,1,0:T(4,128)}, f32[2,4,384,128]{3,2,1,0:T(8,128)}) %tuple.143, (s32[]{:T(128)}, bf16[384,2,128]{2,0,1:T(8,128)(2,1)S(1)}, ...), branch_computations={%region_21.21_spmd, %region_22.0_spmd} | conditional | flops 620697984 | bytes 32787672 | solution.py:29
  297.2 5.6 %conditional.15 = ((f32[2,4,384]{2,1,0:T(4,128)}, f32[2,4,384]{2,1,0:T(4,128)}, f32[2,4,384,128]{3,2,1,0:T(8,128)})) conditional(s32[]{:T(128)} %convert_element_type.163, (f32[2,4,384]{2,1,0:T(4,128)}, f32[2,4,384]{2,1,0:T(4,128)}, f32[2,4,384,128]{3,2,1,0:T(8,128)}) %get-tuple-element.983, (s32[]{:T(128)}, bf16[384,2,128]{2,0,1:T(8,128)(2,1)S(1)}, ...), branch_computations={%region_25.25_spmd, %region_26.0_spmd} | conditional | flops 620697984 | bytes 32787672 | solution.py:29
  307.3 2.5 collective-permute-start
  309.8 4.2 collective-permute-start.1
  315.6 3.2 collective-permute-done.1
  320.6 5.6 %conditional.15 = ((f32[2,4,384]{2,1,0:T(4,128)}, f32[2,4,384]{2,1,0:T(4,128)}, f32[2,4,384,128]{3,2,1,0:T(8,128)})) conditional(s32[]{:T(128)} %convert_element_type.163, (f32[2,4,384]{2,1,0:T(4,128)}, f32[2,4,384]{2,1,0:T(4,128)}, f32[2,4,384,128]{3,2,1,0:T(8,128)}) %get-tuple-element.983, (s32[]{:T(128)}, bf16[384,2,128]{2,0,1:T(8,128)(2,1)S(1)}, ...), branch_computations={%region_25.25_spmd, %region_26.0_spmd} | conditional | flops 620697984 | bytes 32787672 | solution.py:29
  334.7 11.5 %fusion.111 = f32[768,4096]{1,0:T(8,128)} fusion(bf16[768,128,4,2]{1,0,3,2:T(8,128)(2,1)S(1)} %bitcast.309, bf16[2,4,128,4096]{3,2,1,0:T(8,128)(2,1)} %bitcast.326), kind=kOutput, calls=%fused_computation.140 | convolution fusion | flops 6442450944 | bytes 22544384 | tf_op jit(solution)/shard_map/ahgqd,hgde->aqe/dot_general | solution.py:74
  346.3 124.4 %reduce-scatter.2.cloned.1.call-done = f32[192,4096]{1,0:T(8,128)} async-done(((f32[768,4096]{1,0:T(8,128)}), f32[192,4096]{1,0:T(8,128)}) %reduce-scatter.2.cloned.1.call-update) | async-done | bytes 3145744 | tf_op jit(solution)/shard_map/reduce_scatter | solution.py:75
  470.7 3.2 convert_element_type.115
  (353 shorter events, 133.7 us)
Async XLA Ops:
  6.5 69.3 %all-gather.2.cloned.1.call-start = ((), (), s32[]{:S(2)}) async-start(), calls=%async_computation.1 | async-start | bytes 7864320 | tf_op jit(solution)/shard_map/all_gather | solution.py:37
  7.3 463.4 %reduce-scatter.2.cloned.1.call-start = ((), (), s32[]{:S(2)}) async-start(), calls=%async_computation.2 | async-start | bytes 15728640 | tf_op jit(solution)/shard_map/reduce_scatter | solution.py:75
  95.6 9.8 %copy-start.14 = (bf16[384,256]{0,1:T(8,128)(2,1)}, bf16[384,256]{0,1:T(8,128)(2,1)S(1)}, u32[]{:S(2)}) copy-start(bf16[384,256]{0,1:T(8,128)(2,1)S(1)} %get-tuple-element.759) | copy-start | bytes 589828
  96.5 7.5 %copy-start.9 = (bf16[384,1024]{1,0:T(8,128)(2,1)S(1)}, bf16[384,1024]{1,0:T(8,128)(2,1)}, u32[]{:S(2)}) copy-start(bf16[384,1024]{1,0:T(8,128)(2,1)} %get-tuple-element.754) | copy-start | bytes 2359300
  105.4 3.8 copy-start
  105.4 3.8 copy-start.4
  115.9 11.8 %copy-start.1 = (f32[2,4,384]{2,1,0:T(4,128)}, f32[2,4,384]{2,1,0:T(4,128)S(1)}, u32[]{:S(2)}) copy-start(f32[2,4,384]{2,1,0:T(4,128)S(1)} %max.19) | copy-start | bytes 36868
  115.9 6.4 %copy-start.27 = (bf16[384,256]{0,1:T(8,128)(2,1)S(1)}, bf16[384,256]{0,1:T(8,128)(2,1)}, u32[]{:S(2)}) copy-start(bf16[384,256]{0,1:T(8,128)(2,1)} %get-tuple-element.757) | copy-start | bytes 589828
  115.9 11.8 %slice-start = ((s8[4718592]{0:T(1024)(128)(4,1)}), s8[4194304]{0:T(1024)(128)(4,1)S(1)}, s32[]{:S(2)}) async-start(s8[4718592]{0:T(1024)(128)(4,1)} %bitcast.290), calls=%async_computation.3 | async-start | bytes 8388608
  122.4 5.4 %slice-start.1 = ((s8[4718592]{0:T(1024)(128)(4,1)}), s8[524288]{0:T(1024)(128)(4,1)S(1)}, s32[]{:S(2)}) async-start(s8[4718592]{0:T(1024)(128)(4,1)} %bitcast.290), calls=%async_computation.4 | async-start | bytes 1048576
  122.4 5.4 %copy-start.15 = (bf16[384,256]{0,1:T(8,128)(2,1)S(1)}, bf16[384,256]{0,1:T(8,128)(2,1)}, u32[]{:S(2)}) copy-start(bf16[384,256]{0,1:T(8,128)(2,1)} %copy-done.14) | copy-start | bytes 589828
  122.4 5.4 %copy-start.26 = (bf16[384,256]{0,1:T(8,128)(2,1)S(1)}, bf16[384,256]{0,1:T(8,128)(2,1)}, u32[]{:S(2)}) copy-start(bf16[384,256]{0,1:T(8,128)(2,1)} %get-tuple-element.756) | copy-start | bytes 589828
  131.8 12.8 %collective-permute-start = (bf16[2,384,2,128]{3,1,2,0:T(8,128)(2,1)}, bf16[2,384,2,128]{3,1,2,0:T(8,128)(2,1)}, u32[]{:S(2)}, u32[]{:S(2)}) collective-permute-start(bf16[2,384,2,128]{3,1,2,0:T(8,128)(2,1)} %get-tuple-element.941), channel_id=1, source_target_pairs={{0,1},{1,2},{2,3},{3,4},{4,5},{5,6},{6,7},{7,0},{8,9},{9,10},{10,1... | collective-permute-start | bytes 1179656 | tf_op jit(solution)/shard_map/while/body/eval_jaxpr/ppermute | solution.py:67
  139.9 8.9 %collective-permute-start.1 = (bf16[2,384,2,128]{3,1,2,0:T(8,128)(2,1)}, bf16[2,384,2,128]{3,1,2,0:T(8,128)(2,1)}, u32[]{:S(2)}, u32[]{:S(2)}) collective-permute-start(bf16[2,384,2,128]{3,1,2,0:T(8,128)(2,1)} %get-tuple-element.942), channel_id=1, source_target_pairs={{0,1},{1,2},{2,3},{3,4},{4,5},{5,6},{6,7},{7,0},{8,9},{9,10},{10,1... | collective-permute-start | bytes 1179656 | tf_op jit(solution)/shard_map/while/body/eval_jaxpr/ppermute | solution.py:67
  150.7 6.9 %copy-start.5 = (bf16[384,2,128]{2,0,1:T(8,128)(2,1)S(1)}, bf16[384,2,128]{2,0,1:T(8,128)(2,1)}, u32[]{:S(2)}) copy-start(bf16[384,2,128]{2,0,1:T(8,128)(2,1)} %get-tuple-element.873) | copy-start | bytes 589828 | tf_op jit(solution)/shard_map/while
  150.8 3.4 copy-start.8
  150.8 3.4 copy-start.22
  161.1 8.1 %collective-permute-start = (bf16[2,384,2,128]{3,1,2,0:T(8,128)(2,1)}, bf16[2,384,2,128]{3,1,2,0:T(8,128)(2,1)}, u32[]{:S(2)}, u32[]{:S(2)}) collective-permute-start(bf16[2,384,2,128]{3,1,2,0:T(8,128)(2,1)} %get-tuple-element.941), channel_id=1, source_target_pairs={{0,1},{1,2},{2,3},{3,4},{4,5},{5,6},{6,7},{7,0},{8,9},{9,10},{10,1... | collective-permute-start | bytes 1179656 | tf_op jit(solution)/shard_map/while/body/eval_jaxpr/ppermute | solution.py:67
  163.6 9.4 %collective-permute-start.1 = (bf16[2,384,2,128]{3,1,2,0:T(8,128)(2,1)}, bf16[2,384,2,128]{3,1,2,0:T(8,128)(2,1)}, u32[]{:S(2)}, u32[]{:S(2)}) collective-permute-start(bf16[2,384,2,128]{3,1,2,0:T(8,128)(2,1)} %get-tuple-element.942), channel_id=1, source_target_pairs={{0,1},{1,2},{2,3},{3,4},{4,5},{5,6},{6,7},{7,0},{8,9},{9,10},{10,1... | collective-permute-start | bytes 1179656 | tf_op jit(solution)/shard_map/while/body/eval_jaxpr/ppermute | solution.py:67
  177.1 2.2 copy-start.11
  180.6 2.1 copy-start.6
  180.6 2.1 copy-start.18
  182.7 2.2 copy-start.13
  190.5 8.8 %collective-permute-start = (bf16[2,384,2,128]{3,1,2,0:T(8,128)(2,1)}, bf16[2,384,2,128]{3,1,2,0:T(8,128)(2,1)}, u32[]{:S(2)}, u32[]{:S(2)}) collective-permute-start(bf16[2,384,2,128]{3,1,2,0:T(8,128)(2,1)} %get-tuple-element.941), channel_id=1, source_target_pairs={{0,1},{1,2},{2,3},{3,4},{4,5},{5,6},{6,7},{7,0},{8,9},{9,10},{10,1... | collective-permute-start | bytes 1179656 | tf_op jit(solution)/shard_map/while/body/eval_jaxpr/ppermute | solution.py:67
  190.5 11.7 %collective-permute-start.1 = (bf16[2,384,2,128]{3,1,2,0:T(8,128)(2,1)}, bf16[2,384,2,128]{3,1,2,0:T(8,128)(2,1)}, u32[]{:S(2)}, u32[]{:S(2)}) collective-permute-start(bf16[2,384,2,128]{3,1,2,0:T(8,128)(2,1)} %get-tuple-element.942), channel_id=1, source_target_pairs={{0,1},{1,2},{2,3},{3,4},{4,5},{5,6},{6,7},{7,0},{8,9},{9,10},{10,1... | collective-permute-start | bytes 1179656 | tf_op jit(solution)/shard_map/while/body/eval_jaxpr/ppermute | solution.py:67
  204.2 2.1 copy-start.7
  204.3 2.1 copy-start.16
  206.4 2.2 copy-start.11
  212.0 2.2 copy-start.13
  219.8 9.7 %collective-permute-start = (bf16[2,384,2,128]{3,1,2,0:T(8,128)(2,1)}, bf16[2,384,2,128]{3,1,2,0:T(8,128)(2,1)}, u32[]{:S(2)}, u32[]{:S(2)}) collective-permute-start(bf16[2,384,2,128]{3,1,2,0:T(8,128)(2,1)} %get-tuple-element.941), channel_id=1, source_target_pairs={{0,1},{1,2},{2,3},{3,4},{4,5},{5,6},{6,7},{7,0},{8,9},{9,10},{10,1... | collective-permute-start | bytes 1179656 | tf_op jit(solution)/shard_map/while/body/eval_jaxpr/ppermute | solution.py:67
  222.3 8.9 %collective-permute-start.1 = (bf16[2,384,2,128]{3,1,2,0:T(8,128)(2,1)}, bf16[2,384,2,128]{3,1,2,0:T(8,128)(2,1)}, u32[]{:S(2)}, u32[]{:S(2)}) collective-permute-start(bf16[2,384,2,128]{3,1,2,0:T(8,128)(2,1)} %get-tuple-element.942), channel_id=1, source_target_pairs={{0,1},{1,2},{2,3},{3,4},{4,5},{5,6},{6,7},{7,0},{8,9},{9,10},{10,1... | collective-permute-start | bytes 1179656 | tf_op jit(solution)/shard_map/while/body/eval_jaxpr/ppermute | solution.py:67
  233.2 2.1 copy-start.7
  233.2 2.1 copy-start.16
  235.3 2.2 copy-start.11
  238.8 2.1 copy-start.6
  238.9 2.1 copy-start.18
  241.0 2.2 copy-start.13
  248.8 10.9 %collective-permute-start = (bf16[2,384,2,128]{3,1,2,0:T(8,128)(2,1)}, bf16[2,384,2,128]{3,1,2,0:T(8,128)(2,1)}, u32[]{:S(2)}, u32[]{:S(2)}) collective-permute-start(bf16[2,384,2,128]{3,1,2,0:T(8,128)(2,1)} %get-tuple-element.941), channel_id=1, source_target_pairs={{0,1},{1,2},{2,3},{3,4},{4,5},{5,6},{6,7},{7,0},{8,9},{9,10},{10,1... | collective-permute-start | bytes 1179656 | tf_op jit(solution)/shard_map/while/body/eval_jaxpr/ppermute | solution.py:67
  251.3 9.4 %collective-permute-start.1 = (bf16[2,384,2,128]{3,1,2,0:T(8,128)(2,1)}, bf16[2,384,2,128]{3,1,2,0:T(8,128)(2,1)}, u32[]{:S(2)}, u32[]{:S(2)}) collective-permute-start(bf16[2,384,2,128]{3,1,2,0:T(8,128)(2,1)} %get-tuple-element.942), channel_id=1, source_target_pairs={{0,1},{1,2},{2,3},{3,4},{4,5},{5,6},{6,7},{7,0},{8,9},{9,10},{10,1... | collective-permute-start | bytes 1179656 | tf_op jit(solution)/shard_map/while/body/eval_jaxpr/ppermute | solution.py:67
  264.8 2.2 copy-start.11
  270.5 2.2 copy-start.13
  278.3 7.0 %collective-permute-start = (bf16[2,384,2,128]{3,1,2,0:T(8,128)(2,1)}, bf16[2,384,2,128]{3,1,2,0:T(8,128)(2,1)}, u32[]{:S(2)}, u32[]{:S(2)}) collective-permute-start(bf16[2,384,2,128]{3,1,2,0:T(8,128)(2,1)} %get-tuple-element.941), channel_id=1, source_target_pairs={{0,1},{1,2},{2,3},{3,4},{4,5},{5,6},{6,7},{7,0},{8,9},{9,10},{10,1... | collective-permute-start | bytes 1179656 | tf_op jit(solution)/shard_map/while/body/eval_jaxpr/ppermute | solution.py:67
  280.6 9.2 %collective-permute-start.1 = (bf16[2,384,2,128]{3,1,2,0:T(8,128)(2,1)}, bf16[2,384,2,128]{3,1,2,0:T(8,128)(2,1)}, u32[]{:S(2)}, u32[]{:S(2)}) collective-permute-start(bf16[2,384,2,128]{3,1,2,0:T(8,128)(2,1)} %get-tuple-element.942), channel_id=1, source_target_pairs={{0,1},{1,2},{2,3},{3,4},{4,5},{5,6},{6,7},{7,0},{8,9},{9,10},{10,1... | collective-permute-start | bytes 1179656 | tf_op jit(solution)/shard_map/while/body/eval_jaxpr/ppermute | solution.py:67
  293.9 2.2 copy-start.11
  299.5 2.2 copy-start.13
  307.3 7.2 %collective-permute-start = (bf16[2,384,2,128]{3,1,2,0:T(8,128)(2,1)}, bf16[2,384,2,128]{3,1,2,0:T(8,128)(2,1)}, u32[]{:S(2)}, u32[]{:S(2)}) collective-permute-start(bf16[2,384,2,128]{3,1,2,0:T(8,128)(2,1)} %get-tuple-element.941), channel_id=1, source_target_pairs={{0,1},{1,2},{2,3},{3,4},{4,5},{5,6},{6,7},{7,0},{8,9},{9,10},{10,1... | collective-permute-start | bytes 1179656 | tf_op jit(solution)/shard_map/while/body/eval_jaxpr/ppermute | solution.py:67
  309.8 8.9 %collective-permute-start.1 = (bf16[2,384,2,128]{3,1,2,0:T(8,128)(2,1)}, bf16[2,384,2,128]{3,1,2,0:T(8,128)(2,1)}, u32[]{:S(2)}, u32[]{:S(2)}) collective-permute-start(bf16[2,384,2,128]{3,1,2,0:T(8,128)(2,1)} %get-tuple-element.942), channel_id=1, source_target_pairs={{0,1},{1,2},{2,3},{3,4},{4,5},{5,6},{6,7},{7,0},{8,9},{9,10},{10,1... | collective-permute-start | bytes 1179656 | tf_op jit(solution)/shard_map/while/body/eval_jaxpr/ppermute | solution.py:67
  322.9 2.2 copy-start.13
  (54 other events, 84.5 us)
Sparse Core Ops, SparseCore 0:
  8.9 66.8 all-gather.1
  346.4 124.2 reduce-scatter.1
where the time goes:
time: 483 us; the launch traced here: 481 us
  waiting for transfers between devices  227 us (47%)
  matrix products  83.7 us (17%)
  local copies, waits for them, and re-layouts  78.2 us (16%)
  starting transfers between devices  45.5 us (9%)
  other arithmetic  31.4 us (7%)
  between operations  13.6 us (3%)
    reduce_scatter x1, waiting for transfers between devices, local_attn(): y_rows = lax.psum_scatter(part_sum, 'tp', scatter_dimension=0, tiled=True)  124 us
    all_gather x1, waiting for transfers between devices, local_attn(): x_block = lax.all_gather(x_part, 'tp', axis=0, tiled=True)  68.4 us
    ppermute x14, starting transfers between devices, ring_free_step(): k_blocks, v_blocks = lax.ppermute((k_blocks, v_blocks), 'sp', next_pairs)  45.4 us
    dot_general x14, matrix products, block_update(): jnp.einsum('hgqk,khd->hgqd', prob_blk.astype(jnp.bfloat16), v_blk, prefer...  35.1 us
    ppermute x14, waiting for transfers between devices, ring_free_step(): k_blocks, v_blocks = lax.ppermute((k_blocks, v_blocks), 'sp', next_pairs)  33.4 us
    while x28, local copies, waits for them, and re-layouts  30.3 us
    reduce_sum x13, other arithmetic, block_update(): new_sum = row_sum * rescale + jnp.sum(prob_blk, axis=-1)  18.9 us
    dot_general x14, matrix products, block_update(): jnp.einsum('qhgd,khd->hgqk', q_blk, k_blk, preferred_element_type=jnp.flo...  15.4 us
  transfers between devices with their start and end apart: 16, of which 15 were waited for; matrix products, arithmetic and copies ran while one was open for 2% of the time, Pallas kernels for 0%

commit v1 on v0

v1 whole, which is shorter than its diff:
```python
import functools

import jax
import jax.numpy as jnp
from jax import lax
from jax.experimental import pallas as pl
from jax.experimental.pallas import tpu as pltpu
from jax.sharding import PartitionSpec as P

WINDOW = 4096
NEG_BIG = -1e30
LOG2E = 1.4426950408889634
TILE = 256
MESH = pl.DeviceIdType.MESH
NT = (((1,), (1,)), ((), ()))
NN = (((1,), (0,)), ((), ()))


def attn_kernel(dims, q_ref, kv_in, o_ref, kv, m_s, l_s, acc_s, own_sem, send_sem, recv_sem):
    sp_size, chunk, head_dim, kv_loc, group = dims
    chips = sp_size // 2
    cols = group * chunk
    tiles = cols // TILE
    scale = head_dim ** -0.5 * LOG2E
    me = lax.axis_index("sp")
    core = lax.rem(me, 2)
    chip = me // 2

    def rank(dx, flip):
        c = core if flip == 0 else 1 - core
        return 2 * lax.rem(chip + dx + chips, chips) + c

    partner, right, left = rank(0, 1), rank(1, 0), rank(-1, 0)
    own = pltpu.make_async_copy(kv_in, kv.at[me], own_sem)
    own.start()
    barrier = pltpu.get_barrier_semaphore()
    for peer in (partner, right, left):
        pl.semaphore_signal(barrier, inc=1, device_id={"sp": peer}, device_id_type=MESH)
    pl.semaphore_wait(barrier, 3)

    def piece(src, half, peer, slot):
        return pltpu.make_async_remote_copy(
            src_ref=kv.at[src, half],
            dst_ref=kv.at[src, half],
            send_sem=send_sem.at[slot],
            recv_sem=recv_sem.at[src, half],
            device_id={"sp": peer},
            device_id_type=MESH,
        )

    own.wait()
    opp = rank(2, 0)
    sends = [
        piece(me, 0, right, 0), piece(me, 1, left, 1),
        piece(me, 0, partner, 2), piece(me, 1, partner, 3),
        piece(me, 1, right, 4), piece(me, 0, left, 5),
        piece(left, 0, right, 6), piece(right, 1, left, 7),
        piece(left, 0, partner, 8), piece(right, 1, partner, 9),
        piece(left, 1, partner, 10), piece(right, 0, partner, 11),
        piece(opp, 0, partner, 12), piece(opp, 1, partner, 13),
    ]
    for s in sends[:6]:
        s.start()

    m_s[...] = jnp.full(m_s.shape, NEG_BIG, jnp.float32)
    l_s[...] = jnp.zeros_like(l_s)
    acc_s[...] = jnp.zeros_like(acc_s)

    def update(a, src, b, gap, masked):
        for g in range(kv_loc):
            k_blk = kv[src, b, g * chunk:(g + 1) * chunk, :]
            base = kv_loc * chunk
            parts = [kv[src, b, base + (j * kv_loc + g) * head_dim:base + (j * kv_loc + g + 1) * head_dim, :] for j in range(chunk // 128)]
            v_t = jnp.concatenate(parts, axis=1)
            for t in range(tiles):
                s = lax.dot_general(k_blk, q_ref[a, g, t * TILE:(t + 1) * TILE, :], NT, preferred_element_type=jnp.float32)
                if masked:
                    low = (t * TILE) // chunk * chunk
                    base_col = t * TILE - low
                    raw = base_col + lax.broadcasted_iota(jnp.int32, (chunk, TILE), 1)
                    q_pos = jnp.where(raw >= chunk, raw - chunk, raw)
                    off = gap * chunk + q_pos - lax.broadcasted_iota(jnp.int32, (chunk, TILE), 0)
                    s = jnp.where((off >= 0) & (off < WINDOW), s, NEG_BIG)
                m_old = m_s[a, g, t]
                m_new = jnp.maximum(m_old, jnp.max(s, axis=0, keepdims=True))
                p = jnp.exp2((s - m_new) * scale)
                alpha = jnp.exp2((m_old - m_new) * scale)
                m_s[a, g, t] = m_new
                l_s[a, g, t] = l_s[a, g, t] * alpha + jnp.sum(p, axis=0, keepdims=True)
                acc_s[a, g, t] = acc_s[a, g, t] * alpha + lax.dot_general(v_t, p.astype(jnp.bfloat16), NN, preferred_element_type=jnp.float32)

    q_ids = (me, 2 * sp_size - 1 - me)
    order = [(0, 0, 0), (0, 0, 1), (0, 1, 0), (0, 1, 1), (-1, 0, 0), (1, 0, 1), (-1, 1, 0), (1, 1, 1),
             (-1, 0, 1), (1, 0, 0), (-1, 1, 1), (1, 1, 0), (2, 0, 0), (2, 0, 1), (2, 1, 0), (2, 1, 1)]
    forwards = {4: (6, 8), 5: (7, 9), 8: (10,), 9: (11,), 12: (12,), 13: (13,)}

    def pick(i, field):
        out = 0
        for n, entry in enumerate(order):
            if entry[field]:
                out = out + jnp.where(i == n, entry[field], 0)
        return out

    def item(i, carry):
        dx, flip, b = pick(i, 0), pick(i, 1), pick(i, 2)
        src_core = core + flip - 2 * core * flip
        src = 2 * lax.rem(chip + dx + chips, chips) + src_core

        @pl.when(i >= 2)
        def _():
            pltpu.make_async_remote_copy(
                src_ref=kv.at[src, b], dst_ref=kv.at[src, b], send_sem=send_sem.at[0], recv_sem=recv_sem.at[src, b],
                device_id={"sp": partner}, device_id_type=MESH).wait_recv()

        for n, slots in forwards.items():
            @pl.when(i == n)
            def _():
                for slot in slots:
                    sends[slot].start()

        k_id = b * (2 * sp_size - 1) + (1 - 2 * b) * src
        for a in range(2):
            gap = q_ids[a] - k_id
            needed = (gap >= 0) & (gap * chunk - chunk + 1 < WINDOW)
            masked = (gap == 0) | (gap * chunk + chunk - 1 >= WINDOW)

            @pl.when(needed & masked)
            def _():
                update(a, src, b, gap, True)

            @pl.when(needed & jnp.logical_not(masked))
            def _():
                update(a, src, b, gap, False)

        return carry

    lax.fori_loop(0, len(order), item, 0)

    for a in range(2):
        for g in range(kv_loc):
            norm = [acc_s[a, g, t] * (1.0 / l_s[a, g, t]) for t in range(tiles)]
            for t in range(tiles):
                for u in range(TILE // 128):
                    col = t * TILE + u * 128
                    h, row = g * group + col // chunk, col % chunk
                    o_ref[a * chunk + row:a * chunk + row + 128, h * head_dim:(h + 1) * head_dim] = norm[t][:, u * 128:(u + 1) * 128].T.astype(jnp.bfloat16)
    for s in sends:
        s.wait_send()


def attention(sp_size, q, kv):
    _, kv_loc, cols, head_dim = q.shape
    chunk = kv.shape[1] // (2 * kv_loc)
    group = cols // chunk
    tiles = cols // TILE
    return pl.pallas_call(
        functools.partial(attn_kernel, (sp_size, chunk, head_dim, kv_loc, group)),
        name="ring_attention",
        out_shape=jax.ShapeDtypeStruct((2 * chunk, kv_loc * group * head_dim), jnp.bfloat16),
        in_specs=[pl.BlockSpec(memory_space=pltpu.VMEM), pl.BlockSpec(memory_space=pl.ANY)],
        out_specs=pl.BlockSpec(memory_space=pltpu.VMEM),
        scratch_shapes=[
            pltpu.VMEM((sp_size,) + kv.shape, jnp.bfloat16),
            pltpu.VMEM((2, kv_loc, tiles, 1, TILE), jnp.float32),
            pltpu.VMEM((2, kv_loc, tiles, 1, TILE), jnp.float32),
            pltpu.VMEM((2, kv_loc, tiles, head_dim, TILE), jnp.float32),
            pltpu.SemaphoreType.DMA,
            pltpu.SemaphoreType.DMA((14,)),
            pltpu.SemaphoreType.DMA((sp_size, 2)),
        ],
        compiler_params=pltpu.CompilerParams(collective_id=1, has_side_effects=True, vmem_limit_bytes=56 << 20),
    )(q, kv)


def solution(mesh):
    sp_size = mesh.shape["sp"]

    def local_attn(x_part, w_query, w_key, w_value, w_out):
        x_block = lax.all_gather(x_part, "tp", axis=0, tiled=True)
        block_rows, d_model = x_block.shape
        chunk = block_rows // 2
        heads_loc, head_dim = w_query.shape[1], w_query.shape[2]
        kv_loc = w_key.shape[1]
        group = heads_loc // kv_loc

        def project(w):
            return jnp.dot(x_block, w.reshape(d_model, -1), preferred_element_type=jnp.float32).astype(jnp.bfloat16)

        q = project(w_query).reshape(2, chunk, kv_loc, group, head_dim).transpose(0, 2, 3, 1, 4).reshape(2, kv_loc, group * chunk, head_dim)
        k = project(w_key).reshape(2, chunk, kv_loc, head_dim).transpose(0, 2, 1, 3).reshape(2, kv_loc * chunk, head_dim)
        v = project(w_value).reshape(2, chunk // 128, 128, kv_loc, head_dim).transpose(0, 1, 3, 4, 2).reshape(2, kv_loc * chunk, 128)
        o = attention(sp_size, q, jnp.concatenate([k, v], axis=1))
        part_sum = jnp.dot(o, w_out.reshape(heads_loc * head_dim, d_model), preferred_element_type=jnp.float32)
        y_rows = lax.psum_scatter(part_sum, "tp", scatter_dimension=0, tiled=True)
        return y_rows.astype(jnp.bfloat16)

    return jax.shard_map(local_attn, mesh=mesh, in_specs=(P(("dp", "sp", "tp"), None), P(None, "tp", None), P(None, "tp", None), P(None, "tp", None), P("tp", None, None)), out_specs=P(("dp", "sp", "tp"), None), check_vma=False)
```

time: 483 us -> 319 us (0.66)
  local copies, waits for them, and re-layouts: 78.2 us -> 3.96 us
  Pallas kernels: 0 us -> 70.5 us
  matrix products: 83.7 us -> 33.1 us
  starting transfers between devices: 45.5 us -> 0.06 us
  waiting for transfers between devices: 227 us -> 194 us
  other arithmetic: 31.4 us -> 4.18 us
    pallas_call x0 -> x1, Pallas kernels: none -> 70.5 us  [attention(): pl.pallas_call(functools.partial(attn_kernel, (sp_size, chunk, head_dim,...]
    dot_general x32 -> x4, matrix products: 83.7 us -> 33.1 us  [the longest x3 21 us: project(): jnp.dot(x_block, w.reshape(d_model, -1), preferred_element_type=jnp.float32)]
    ppermute x14 -> x0, starting transfers between devices: 45.4 us -> none  [ring_free_step(): k_blocks, v_blocks = lax.ppermute((k_blocks, v_blocks), 'sp', next_pairs)]
    while x31 -> x0, local copies, waits for them, and re-layouts: 34.4 us -> none
    ppermute x14 -> x0, waiting for transfers between devices: 33.4 us -> none  [ring_free_step(): k_blocks, v_blocks = lax.ppermute((k_blocks, v_blocks), 'sp', next_pairs)]
    squeeze x23 -> x0, local copies, waits for them, and re-layouts: 21.9 us -> none  [the longest x7 12.7 us: absorb(): v_blocks[k_half]]
    reduce_sum x13 -> x0, other arithmetic: 18.9 us -> none  [block_update(): new_sum = row_sum * rescale + jnp.sum(prob_blk, axis=-1)]
    cond x150 -> x0, local copies, waits for them, and re-layouts: 14 us -> none
  transfers between devices with their start and end apart: 16 -> 2, of which waited for: 15 -> 2; matrix products, arithmetic and copies ran while one was open for 2% -> 0% of each run, Pallas kernels for 0% -> 0%
where the time goes in v1:
time: 319 us
  waiting for transfers between devices  194 us (61%)
  Pallas kernels  70.5 us (22%)
  matrix products  33.1 us (10%)
  between operations  13.5 us (4%)
  other arithmetic  4.18 us (1%)
  local copies, waits for them, and re-layouts  3.96 us (1%)
    reduce_scatter x1, waiting for transfers between devices, local_attn(): y_rows = lax.psum_scatter(part_sum, 'tp', scatter_dimension=0, tiled=True)  125 us
    pallas_call x1, Pallas kernels, attention(): pl.pallas_call(functools.partial(attn_kernel, (sp_size, chunk, head_dim,...  70.5 us
    all_gather x1, waiting for transfers between devices, local_attn(): x_block = lax.all_gather(x_part, 'tp', axis=0, tiled=True)  68.4 us
    dot_general x3, matrix products, project(): jnp.dot(x_block, w.reshape(d_model, -1), preferred_element_type=jnp.float32)  21 us
    dot_general x1, matrix products, local_attn(): jnp.dot(o, w_out.reshape(heads_loc * head_dim, d_model), preferred_elemen...  12.2 us
  transfers between devices with their start and end apart: 2, of which 2 were waited for; matrix products, arithmetic and copies ran while one was open for 0% of the time, Pallas kernels for 0%

profile of v1, /device:TPU:97, one launch (start us, length us, event | category | flops | bytes accessed | tf_op | source)
XLA Modules:
  0.0 319.2 jit_solution(9531454293103466060)
XLA Ops:
  6.5 0.0 all-gather.2.cloned.1.call-start
  6.6 0.7 all-gather.2.cloned.1.call-update
  7.3 0.1 reduce-scatter.2.cloned.1.call-start
  7.4 68.4 %all-gather.2.cloned.1.call-done = bf16[768,4096]{1,0:T(8,128)(2,1)} async-done(((bf16[192,4096]{1,0:T(8,128)(2,1)}), bf16[768,4096]{1,0:T(8,128)(2,1)}) %all-gather.2.cloned.1.call-update) | async-done | bytes 6291472 | tf_op jit(solution)/shard_map/all_gather | solution.py:179
  75.8 5.2 %fusion.15 = bf16[768,256]{1,0:T(8,128)(2,1)S(1)} fusion(bf16[768,4096]{1,0:T(8,128)(2,1)} %all-gather.2.cloned.1.call-done, bf16[512,8,2,128]{3,2,1,0:T(2,128)(2,1)} %bitcast.38), kind=kOutput, calls=%fused_computation.11 | convolution fusion | flops 1610809344 | bytes 8781824 | tf_op jit(solution)/shard_map/dot_general | solution.py:187
  81.0 0.1 reshape.37
  81.1 0.4 copy.8
  81.5 11.2 %fusion.9 = bf16[768,1024]{1,0:T(8,128)(2,1)S(1)} fusion(bf16[768,4096]{1,0:T(8,128)(2,1)} %all-gather.2.cloned.1.call-done, bf16[512,8,8,128]{3,2,1,0:T(8,128)(2,1)} %bitcast.36), kind=kOutput, calls=%fused_computation.9 | convolution fusion | flops 6443237376 | bytes 16252928 | tf_op jit(solution)/shard_map/dot_general | solution.py:187
  92.7 1.1 reshape.31
  93.9 0.0 copy-start
  93.9 1.4 copy.6
  95.3 0.8 copy-done
  96.0 4.6 %fusion.12 = bf16[768,256]{1,0:T(8,128)(2,1)S(1)} fusion(bf16[768,4096]{1,0:T(8,128)(2,1)} %all-gather.2.cloned.1.call-done, bf16[512,8,2,128]{3,2,1,0:T(2,128)(2,1)S(1)} %bitcast.39), kind=kOutput, calls=%fused_computation.10 | convolution fusion | flops 1610809344 | bytes 8781824 | tf_op jit(solution)/shard_map/dot_general | solution.py:187
  100.6 0.1 reshape.34
  100.7 0.1 copy.7
  100.8 0.9 pad_maximum_fusion.kv_in
  101.7 70.5 %ring_attention.1 = bf16[768,1024]{1,0:T(8,128)(2,1)} custom-call(bf16[2,2,1536,128]{3,2,1,0:T(8,128)(2,1)} %bitcast.33, bf16[2,1536,128]{2,1,0:T(8,128)(2,1)} %pad_maximum_fusion.kv_in), custom_call_target="tpu_custom_call" | custom-call | tf_op jit(solution)/shard_map/ring_attention/pallas_call | solution.py:156
  172.3 12.2 %fusion.18 = f32[768,4096]{1,0:T(8,128)} fusion(bf16[768,1024]{1,0:T(8,128)(2,1)} %ring_attention.1, bf16[1024,4096]{1,0:T(8,128)(2,1)} %bitcast.37), kind=kOutput, calls=%fused_computation.13 | convolution fusion | flops 6442450944 | bytes 22544384 | tf_op jit(solution)/shard_map/dot_general | solution.py:193
  184.4 0.1 reduce-scatter.2.cloned.1.call-update
  184.5 124.6 %reduce-scatter.2.cloned.1.call-done = f32[192,4096]{1,0:T(8,128)} async-done(((f32[768,4096]{1,0:T(8,128)}), f32[192,4096]{1,0:T(8,128)}) %reduce-scatter.2.cloned.1.call-update) | async-done | bytes 3145744 | tf_op jit(solution)/shard_map/reduce_scatter | solution.py:194
  309.1 3.2 %convert_element_type.15 = bf16[192,4096]{1,0:T(8,128)(2,1)} convert(f32[192,4096]{1,0:T(8,128)} %reduce-scatter.2.cloned.1.call-done) | non-fusion elementwise | flops 786432 | bytes 4718592 | tf_op jit(solution)/shard_map/convert_element_type | solution.py:195
Async XLA Ops:
  6.5 69.3 %all-gather.2.cloned.1.call-start = ((), (), s32[]{:S(2)}) async-start(), calls=%async_computation.1 | async-start | bytes 7864320 | tf_op jit(solution)/shard_map/all_gather | solution.py:179
  7.3 301.8 %reduce-scatter.2.cloned.1.call-start = ((), (), s32[]{:S(2)}) async-start(), calls=%async_computation.2 | async-start | bytes 15728640 | tf_op jit(solution)/shard_map/reduce_scatter | solution.py:194
  93.9 2.2 copy-start
Sparse Core Ops, SparseCore 0:
  8.9 66.8 all-gather.1
  184.6 124.4 reduce-scatter.1

commit v2 on v0

v2 whole, which is shorter than its diff:
```python
import functools

import jax
import jax.numpy as jnp
from jax import lax
from jax.experimental import pallas as pl
from jax.experimental.pallas import tpu as pltpu
from jax.sharding import PartitionSpec as P

WINDOW = 4096
NEG_BIG = -1e30
LOG2E = 1.4426950408889634
TILE = 256
MESH = pl.DeviceIdType.MESH
NT = (((1,), (1,)), ((), ()))
NN = (((1,), (0,)), ((), ()))
ITEMS = [(dx, flip, b) for dx, flip in ((0, 0), (0, 1), (-1, 0), (1, 0), (-1, 1), (1, 1), (2, 0), (2, 1)) for b in (0, 1)]


def layer_kernel(dims, x_in, wq_in, wkv_in, wo_in, out, xs, wq, wkv, q_s, kv, m_s, l_s, acc_s, s_s, wo, o_s, ob, y_s,
                 load_sem, x_send, x_recv, kv_send, kv_recv, wo_load, wo_send, wo_recv, ob_send, ob_recv, y_send, y_recv, y_store):
    sp_size, tp_size, kv_loc, group, head_dim = dims
    chips = sp_size // 2
    rows, half = 2 * xs.shape[2], xs.shape[2]
    chunk = 2 * rows
    cols = group * chunk
    tiles = cols // TILE
    width = kv_loc * head_dim
    scale = head_dim ** -0.5 * LOG2E
    me, my_tp = lax.axis_index("sp"), lax.axis_index("tp")
    core, chip = lax.rem(me, 2), me // 2

    def rank(dx, flip):
        c = core if flip == 0 else 1 - core
        return 2 * lax.rem(chip + dx + chips, chips) + c

    partner, right, left, opp = rank(0, 1), rank(1, 0), rank(-1, 0), rank(2, 0)
    up, down, far = (lax.rem(my_tp + d, tp_size) for d in (1, tp_size - 1, 2))
    tps = (my_tp, down, up, far)

    loads = [pltpu.make_async_copy(x_in.at[pl.ds(h * half, half)], xs.at[0, h], load_sem.at[h]) for h in (0, 1)]
    loads += [pltpu.make_async_copy(wq_in, wq, load_sem.at[2]), pltpu.make_async_copy(wkv_in, wkv, load_sem.at[3])]
    for c in loads:
        c.start()
    w_rows, w_cols = wo.shape[3], wo.shape[4]

    def columns(quarter):
        return pl.ds(pl.multiple_of((core * chips + quarter) * w_cols, w_cols), w_cols)

    wo_loads = [pltpu.make_async_copy(wo_in.at[pl.ds(h * w_rows, w_rows), columns(lax.rem(chip + d, chips))],
                                      wo.at[my_tp, lax.rem(chip + d, chips), h], wo_load.at[d, h]) for d in range(chips) for h in (0, 1)]
    for c in wo_loads:
        c.start()
    barrier = pltpu.get_barrier_semaphore()
    peers = [{"sp": partner}, {"sp": right}, {"sp": left}, {"tp": up}, {"tp": down}, {"tp": far}]
    for peer in peers:
        pl.semaphore_signal(barrier, inc=1, device_id=peer, device_id_type=MESH)
    pl.semaphore_wait(barrier, len(peers))

    def x_piece(src, h, dst, peer, slot):
        return pltpu.make_async_remote_copy(
            src_ref=xs.at[src, h], dst_ref=xs.at[dst, h], send_sem=x_send.at[slot], recv_sem=x_recv.at[dst, h],
            device_id={"tp": peer}, device_id_type=MESH)

    x_sends = [x_piece(0, 0, 1, up, 0), x_piece(0, 1, 1, down, 1), x_piece(0, 1, 2, up, 2), x_piece(0, 0, 2, down, 3),
               x_piece(1, 0, 3, up, 4), x_piece(1, 1, 3, down, 5)]
    owners = ((my_tp, my_tp), (down, up), (up, down), (far, far))

    kv_sends = []

    def kv_copy(src, o, peer):
        copy = pltpu.make_async_remote_copy(
            src_ref=kv.at[src, tps[o]], dst_ref=kv.at[src, tps[o]], send_sem=kv_send.at[len(kv_sends)],
            recv_sem=kv_recv.at[src, tps[o]], device_id={"sp": peer}, device_id_type=MESH)
        kv_sends.append(copy)
        return copy

    own_kv = [[kv_copy(me, o, peer) for peer in (right, left, partner)] for o in range(4)]
    left_kv = [[kv_copy(left, o, peer) for peer in ((right, partner) if o < 2 else (partner,))] for o in range(4)]
    right_kv = [[kv_copy(right, o, peer) for peer in ((left, partner) if o >= 2 else (partner,))] for o in range(4)]
    opp_kv = [[kv_copy(opp, o, partner)] for o in range(4)]

    def start(copies):
        for c in copies:
            c.start()

    def kv_wait(src, o):
        pltpu.make_async_remote_copy(
            src_ref=kv.at[src, tps[o]], dst_ref=kv.at[src, tps[o]], send_sem=kv_send.at[0], recv_sem=kv_recv.at[src, tps[o]],
            device_id={"sp": partner}, device_id_type=MESH).wait_recv()

    def pass_on(side, src, orders):
        for o in orders:
            kv_wait(src, o)
            start(side[o])

    wo_sends = []

    def wo_copy(o, dx, h, peer):
        at = (tps[o], lax.rem(chip + dx + chips, chips), h)
        copy = pltpu.make_async_remote_copy(
            src_ref=wo.at[at], dst_ref=wo.at[at], send_sem=wo_send.at[len(wo_sends)], recv_sem=wo_recv.at[at],
            device_id=peer, device_id_type=MESH)
        wo_sends.append(copy)
        return copy

    def wo_wait(o, dx, h):
        at = (tps[o], lax.rem(chip + dx + chips, chips), h)
        pltpu.make_async_remote_copy(
            src_ref=wo.at[at], dst_ref=wo.at[at], send_sem=wo_send.at[0], recv_sem=wo_recv.at[at],
            device_id={"sp": partner}, device_id_type=MESH).wait_recv()

    to_up, to_down, to_right, to_left = {"tp": up}, {"tp": down}, {"sp": right}, {"sp": left}
    wo_first = [wo_copy(0, 0, 0, to_up), wo_copy(0, 0, 1, to_down)]
    wo_second = [wo_copy(0, 0, 1, to_up), wo_copy(0, 0, 0, to_down)]
    wo_third = [wo_copy(1, 0, 0, to_up), wo_copy(2, 0, 1, to_down)]
    wo_side = {(o, h): [wo_copy(o, 0, h, to_right), wo_copy(o, 0, h, to_left)] for o in (1, 2, 3) for h in (0, 1)}
    wo_relay = {o: [wo_copy(o, -1, 0, to_right), wo_copy(o, 1, 1, to_left)] for o in (1, 2, 3)}

    def relay(o):
        wo_wait(o, -1, 0)
        wo_relay[o][0].start()
        wo_wait(o, 1, 1)
        wo_relay[o][1].start()

    def project(step):
        x_rows = xs[step].reshape(rows, xs.shape[3])
        kv_rows = jnp.dot(x_rows, wkv[...], preferred_element_type=jnp.float32).astype(jnp.bfloat16)
        for h in (0, 1):
            kv[me, owners[step][h], h * half:(h + 1) * half, :] = kv_rows[h * half:(h + 1) * half]
        for g in range(kv_loc):
            for hh in range(group):
                if hh % 2:
                    continue
                lane = (g * group + hh) * head_dim
                res = jnp.dot(x_rows, wq[:, lane:lane + 2 * head_dim], preferred_element_type=jnp.float32).astype(jnp.bfloat16)
                for h in (0, 1):
                    tp = owners[step][h]
                    for n in (0, 1):
                        base = pl.multiple_of((hh + n) * chunk + lax.rem(tp, 2) * rows + h * half, half)
                        q_s[tp // 2, g, pl.ds(base, half), :] = res[h * half:(h + 1) * half, n * head_dim:(n + 1) * head_dim]

    loads[0].wait()
    loads[1].wait()
    for c in wo_loads[:2]:
        c.wait()
    start(wo_first)
    start(x_sends[:4])
    m_s[...] = jnp.full(m_s.shape, NEG_BIG, jnp.float32)
    l_s[...] = jnp.zeros_like(l_s)
    acc_s[...] = jnp.zeros_like(acc_s)
    loads[2].wait()
    loads[3].wait()
    def steps(step, carry):
        @pl.when(step == 1)
        def _():
            start(own_kv[0])
            for o, h in ((1, 0), (2, 1)):
                wo_wait(o, 0, h)
                start(wo_side[o, h])
            x_sends[0].wait_recv()
            x_sends[4].start()
            x_sends[1].wait_recv()
            x_sends[5].start()
            start(wo_second)
            start(wo_third)
            pass_on(left_kv, left, (0,))
            pass_on(right_kv, right, (0,))

        @pl.when(step == 2)
        def _():
            x_sends[2].wait_recv()
            x_sends[3].wait_recv()
            pass_on(opp_kv, opp, (0,))
            wo_wait(1, -1, 0)
            wo_relay[1][0].start()
            wo_wait(2, 1, 1)
            wo_relay[2][1].start()

        @pl.when(step == 3)
        def _():
            start(own_kv[1])
            start(own_kv[2])
            x_sends[4].wait_recv()
            x_sends[5].wait_recv()
            pass_on(left_kv, left, (1, 2))
            pass_on(right_kv, right, (1, 2))

        for n in range(4):
            @pl.when(step == n)
            def _():
                project(n)
        return carry

    lax.fori_loop(0, 4, steps, 0)
    start(own_kv[3])

    def update(a, src, b, gap, masked):
        todo = [(g, t) for g in range(kv_loc) for t in range(tiles)]

        def block(lane):
            return kv[src, pl.ds(2 * b, 2), :, lane:lane + head_dim].reshape(chunk, head_dim)

        def scores(n):
            g, t = todo[n]
            s_s[n % 2] = lax.dot_general(block(g * head_dim), q_s[a, g, t * TILE:(t + 1) * TILE, :], NT, preferred_element_type=jnp.float32)

        scores(0)
        v_t = [block(width + g * head_dim).T for g in range(kv_loc)]
        for n, (g, t) in enumerate(todo):
            if n + 1 < len(todo):
                scores(n + 1)
            s = s_s[n % 2]
            if masked:
                raw = t * TILE % chunk + lax.broadcasted_iota(jnp.int32, (chunk, TILE), 1)
                q_pos = jnp.where(raw >= chunk, raw - chunk, raw)
                off = gap * chunk + q_pos - lax.broadcasted_iota(jnp.int32, (chunk, TILE), 0)
                s = jnp.where((off >= 0) & (off < WINDOW), s, NEG_BIG)
            m_old = m_s[a, g, t]
            m_new = jnp.maximum(m_old, jnp.max(s, axis=0, keepdims=True))
            p = jnp.exp2((s - m_new) * scale)
            alpha = jnp.exp2((m_old - m_new) * scale)
            m_s[a, g, t] = m_new
            l_s[a, g, t] = l_s[a, g, t] * alpha + jnp.sum(p, axis=0, keepdims=True)
            acc_s[a, g, t] = acc_s[a, g, t] * alpha + lax.dot_general(v_t[g], p.astype(jnp.bfloat16), NN, preferred_element_type=jnp.float32)

    def wait_all(src):
        for o in range(4):
            kv_wait(src, o)

    def before(i):
        @pl.when(i == 2)
        def _():
            wait_all(partner)
            pass_on(opp_kv, opp, (1, 2))

        @pl.when(i == 4)
        def _():
            pass_on(left_kv, left, (3,))
            pass_on(right_kv, right, (3,))

        @pl.when(i == 8)
        def _():
            wait_all(rank(-1, 1))
            wait_all(rank(1, 1))
            pass_on(opp_kv, opp, (3,))
            for o, h in ((1, 1), (2, 0)):
                wo_wait(o, 0, h)
                start(wo_side[o, h])

        @pl.when(i == 12)
        def _():
            for h in (0, 1):
                wo_wait(3, 0, h)
                start(wo_side[3, h])

        @pl.when(i == 14)
        def _():
            wait_all(rank(2, 1))

    def pick(i, field):
        out = 0
        for n, entry in enumerate(ITEMS):
            if entry[field]:
                out = out + jnp.where(i == n, entry[field], 0)
        return out

    q_ids = (me, 2 * sp_size - 1 - me)

    def item(i, carry):
        before(i)
        dx, flip, b = pick(i, 0), pick(i, 1), pick(i, 2)
        src = 2 * lax.rem(chip + dx + chips, chips) + core + flip - 2 * core * flip
        k_id = b * (2 * sp_size - 1) + (1 - 2 * b) * src
        for a in range(2):
            gap = q_ids[a] - k_id
            needed = (gap >= 0) & (gap * chunk - chunk + 1 < WINDOW)
            masked = (gap == 0) | (gap * chunk + chunk - 1 >= WINDOW)

            @pl.when(needed & masked)
            def _():
                update(a, src, b, gap, True)

            @pl.when(needed & jnp.logical_not(masked))
            def _():
                update(a, src, b, gap, False)

        return carry

    lax.fori_loop(0, len(ITEMS), item, 0)

    for a in range(2):
        for g in range(kv_loc):
            for t in range(tiles):
                norm = acc_s[a, g, t] * (1.0 / l_s[a, g, t])
                for u in range(TILE // 64):
                    col = t * TILE + u * 64
                    h, row = g * group + col // chunk, col % chunk
                    if u % 2 == 0:
                        turned = norm[:, u * 64:u * 64 + 128].T.astype(jnp.bfloat16)
                    o_s[2 * a + row // rows, row % rows:row % rows + 64, h * head_dim:(h + 1) * head_dim] = turned[u % 2 * 64:u % 2 * 64 + 64]

    ob_sends = []

    def ob_copy(src, o, peer):
        copy = pltpu.make_async_remote_copy(
            src_ref=src, dst_ref=ob.at[tps[o], core], send_sem=ob_send.at[len(ob_sends)], recv_sem=ob_recv.at[tps[o], core],
            device_id=peer, device_id_type=MESH)
        ob_sends.append(copy)
        return copy

    ob[my_tp, core] = o_s[my_tp]
    start([ob_copy(o_s.at[tps[o]], 0, {"tp": tps[o]}) for o in (3, 1, 2)])
    start([ob_copy(ob.at[my_tp, core], 0, {"sp": partner})])

    def ob_wait(o, c):
        at = (tps[o], c)
        pltpu.make_async_remote_copy(
            src_ref=ob.at[at], dst_ref=ob.at[at], send_sem=ob_send.at[0], recv_sem=ob_recv.at[at],
            device_id={"sp": partner}, device_id_type=MESH).wait_recv()

    wo_wait(2, -1, 0)
    wo_relay[2][0].start()
    wo_wait(1, 1, 1)
    wo_relay[1][1].start()
    for o in (1, 2, 3):
        ob_wait(o, core)
        start([ob_copy(ob.at[tps[o], core], o, {"sp": partner})])
    for o in range(4):
        ob_wait(o, 1 - core)
    for c in wo_loads[2:]:
        c.wait()

    def y_remote(n, quarter):
        return pltpu.make_async_remote_copy(
            src_ref=y_s.at[n, 1 - core], dst_ref=out.at[:, columns(quarter)], send_sem=y_send.at[n], recv_sem=y_recv.at[n],
            device_id={"sp": partner}, device_id_type=MESH)

    def y_local(n, quarter):
        return pltpu.make_async_copy(y_s.at[n, core], out.at[:, columns(quarter)], y_store.at[n])

    def quarter_of(n):
        return lax.rem(chip + jnp.where(n == 1, chips - 1, jnp.where(n == 2, 1, jnp.where(n == 3, 2, 0))), chips)

    def finish(n, carry):
        @pl.when(n == 1)
        def _():
            relay(3)
            wo_wait(1, -1, 1)
            wo_wait(2, -1, 1)
            wo_wait(3, -1, 1)

        @pl.when(n == 2)
        def _():
            for o in (1, 2, 3):
                wo_wait(o, 1, 0)

        @pl.when(n == 3)
        def _():
            for o in (1, 2, 3):
                for h in (0, 1):
                    wo_wait(o, 2, h)

        quarter = quarter_of(n)
        for part in range(0, w_cols, TILE):
            total = None
            for tp in range(tp_size):
                res = jnp.dot(ob[tp].reshape(2 * rows, 2 * w_rows), wo[tp, quarter, :, :, part:part + TILE].reshape(2 * w_rows, TILE),
                              preferred_element_type=jnp.float32)
                total = res if total is None else total + res
            y_s[n, :, :, part:part + TILE] = total.astype(jnp.bfloat16).reshape(2, rows, TILE)
        y_remote(n, quarter).start()
        y_local(n, quarter).start()
        return carry

    lax.fori_loop(0, chips, finish, 0)
    for n in range(chips):
        y_remote(n, quarter_of(n)).wait()
        y_local(n, quarter_of(n)).wait()
    for c in x_sends + kv_sends + wo_sends + ob_sends:
        c.wait_send()


def layer(sp_size, tp_size, heads, x_part, w_q, w_kv, w_o):
    kv_loc, group, head_dim = heads
    rows, d_model = x_part.shape
    chunk = 2 * rows
    tiles = group * chunk // TILE
    width = kv_loc * head_dim
    chips = sp_size // 2
    quarter = d_model // sp_size
    f32, bf16 = jnp.float32, jnp.bfloat16
    dma = pltpu.SemaphoreType.DMA
    return pl.pallas_call(
        functools.partial(layer_kernel, (sp_size, tp_size) + heads),
        name="layer",
        out_shape=jax.ShapeDtypeStruct(x_part.shape, bf16),
        in_specs=[pl.BlockSpec(memory_space=pl.ANY)] * 4,
        out_specs=pl.BlockSpec(memory_space=pl.ANY),
        scratch_shapes=[
            pltpu.VMEM((4, 2, rows // 2, d_model), bf16),
            pltpu.VMEM(w_q.shape, bf16),
            pltpu.VMEM(w_kv.shape, bf16),
            pltpu.VMEM((2, kv_loc, group * chunk, head_dim), bf16),
            pltpu.VMEM((sp_size, tp_size, rows, 2 * width), bf16),
            pltpu.VMEM((2, kv_loc, tiles, 1, TILE), f32),
            pltpu.VMEM((2, kv_loc, tiles, 1, TILE), f32),
            pltpu.VMEM((2, kv_loc, tiles, head_dim, TILE), f32),
            pltpu.VMEM((2, chunk, TILE), f32),
            pltpu.VMEM((tp_size, chips, 2, w_o.shape[0] // 2, quarter), bf16),
            pltpu.VMEM((tp_size, rows, w_o.shape[0]), bf16),
            pltpu.VMEM((tp_size, 2, rows, w_o.shape[0]), bf16),
            pltpu.VMEM((chips, 2, rows, quarter), bf16),
            dma((4,)), dma((6,)), dma((4, 2)), dma((28,)), dma((sp_size, tp_size)),
            dma((chips, 2)), dma((24,)), dma((tp_size, chips, 2)), dma((7,)), dma((tp_size, 2)), dma((chips,)), dma((chips,)), dma((chips,)),
        ],
        compiler_params=pltpu.CompilerParams(collective_id=1, has_side_effects=True, vmem_limit_bytes=62 << 20),
    )(x_part, w_q, w_kv, w_o)


def solution(mesh):
    sp_size, tp_size = mesh.shape["sp"], mesh.shape["tp"]

    def local_attn(x_part, w_query, w_key, w_value, w_out):
        d_model = x_part.shape[1]
        heads_loc, head_dim = w_query.shape[1], w_query.shape[2]
        kv_loc = w_key.shape[1]
        w_q = w_query.reshape(d_model, -1)
        w_kv = jnp.concatenate([w_key.reshape(d_model, -1), w_value.reshape(d_model, -1)], axis=1)
        w_o = w_out.reshape(-1, d_model)
        return layer(sp_size, tp_size, (kv_loc, heads_loc // kv_loc, head_dim), x_part, w_q, w_kv, w_o)

    return jax.shard_map(local_attn, mesh=mesh, in_specs=(P(("dp", "sp", "tp"), None), P(None, "tp", None), P(None, "tp", None), P(None, "tp", None), P("tp", None, None)), out_specs=P(("dp", "sp", "tp"), None), check_vma=False)
```

time: 483 us -> 189 us (0.39)
  waiting for transfers between devices: 227 us -> 0 us
  Pallas kernels: 0 us -> 172 us
  matrix products: 83.7 us -> 0 us
  local copies, waits for them, and re-layouts: 78.2 us -> 14.4 us
  starting transfers between devices: 45.5 us -> 0 us
  other arithmetic: 31.4 us -> 2.31 us
  between operations: 13.6 us -> 0.01 us
    pallas_call x0 -> x1, Pallas kernels: none -> 172 us  [layer(): pl.pallas_call(functools.partial(layer_kernel, (sp_size, tp_size) + heads...]
    reduce_scatter x1 -> x0, waiting for transfers between devices: 124 us -> none  [local_attn(): y_rows = lax.psum_scatter(part_sum, 'tp', scatter_dimension=0, tiled=True)]
    dot_general x32 -> x0, matrix products: 83.7 us -> none  [the longest x14 35.1 us: block_update(): jnp.einsum('hgqk,khd->hgqd', prob_blk.astype(jnp.bfloat16), v_blk, prefer...]
    all_gather x1 -> x0, waiting for transfers between devices: 68.4 us -> none  [local_attn(): x_block = lax.all_gather(x_part, 'tp', axis=0, tiled=True)]
    ppermute x14 -> x0, starting transfers between devices: 45.4 us -> none  [ring_free_step(): k_blocks, v_blocks = lax.ppermute((k_blocks, v_blocks), 'sp', next_pairs)]
    while x31 -> x0, local copies, waits for them, and re-layouts: 34.4 us -> none
    ppermute x14 -> x0, waiting for transfers between devices: 33.4 us -> none  [ring_free_step(): k_blocks, v_blocks = lax.ppermute((k_blocks, v_blocks), 'sp', next_pairs)]
    squeeze x23 -> x0, local copies, waits for them, and re-layouts: 21.9 us -> none  [the longest x7 12.7 us: absorb(): v_blocks[k_half]]
  transfers between devices with their start and end apart: 16 -> 0, of which waited for: 15 -> 0; matrix products, arithmetic and copies ran while one was open for 2% -> 0% of each run, Pallas kernels for 0% -> 0%
where the time goes in v2:
time: 189 us
  Pallas kernels  172 us (91%)
  local copies, waits for them, and re-layouts  14.4 us (8%)
  other arithmetic  2.31 us (1%)
    pallas_call x1, Pallas kernels, layer(): pl.pallas_call(functools.partial(layer_kernel, (sp_size, tp_size) + heads...  172 us
    unnamed x2, local copies, waits for them, and re-layouts  11.5 us

profile of v2, /device:TPU:97, one launch (start us, length us, event | category | flops | bytes accessed | tf_op | source)
XLA Modules:
  0.0 188.5 jit_solution(1740210462940561632)
XLA Ops:
  0.0 2.9 %copy_bitcast_fusion.1 = (bf16[4096,256]{1,0:T(8,128)(2,1)S(1)}, bf16[4096,256]{1,0:T(8,128)(2,1)S(1)}) fusion(bf16[512,8,2,128]{3,2,1,0:T(2,128)(2,1)} %bitcast.14, bf16[512,8,2,128]{3,2,1,0:T(2,128)(2,1)} %bitcast.15), kind=kLoop, calls=%fused_computation.2 | loop fusion | bytes 8388608 | tf_op jit(solution)/shard_map/reshape | solution.py:429
  2.9 2.3 %pad_maximum_fusion.wkv_in = bf16[4096,512]{1,0:T(8,128)(2,1)} fusion(bf16[4096,256]{1,0:T(8,128)(2,1)S(1)} %get-tuple-element.5, bf16[4096,256]{1,0:T(8,128)(2,1)S(1)} %get-tuple-element.6), kind=kLoop, calls=%fused_computation.1 | loop fusion | flops 8388608 | bytes 8388608 | tf_op jit(solution)/shard_map/concatenate | solution.py:429
  5.2 8.8 %copy.12 = bf16[512,8,8,128]{3,1,2,0:T(8,128)(2,1)} copy(bf16[512,8,8,128]{3,2,1,0:T(8,128)(2,1)} %bitcast.13) | data formatting | bytes 16777216
  14.0 171.9 %layer.1 = bf16[192,4096]{1,0:T(8,128)(2,1)} custom-call(bf16[192,4096]{1,0:T(8,128)(2,1)} %x_in.1, bf16[4096,1024]{1,0:T(8,128)(2,1)} %bitcast.11, bf16[4096,512]{1,0:T(8,128)(2,1)} %pad_maximum_fusion.wkv_in, bf16[1024,4096]{1,0:T(8,128)(2,1)} %bitcast.12), custom_call_target="tpu_custom_call" | custom-call | tf_op jit(solution)/shard_map/layer/pallas_call | solution.py:394
  185.8 2.7 %copy.14 = bf16[192,4096]{1,0:T(8,128)(2,1)} copy(bf16[192,4096]{1,0:T(8,128)(2,1)} %layer.1) | data formatting | bytes 3145728

commit v3 on v2

--- a/solution.py
+++ b/solution.py
@@ -10,15 +10,20 @@
 WINDOW = 4096
 NEG_BIG = -1e30
 LOG2E = 1.4426950408889634
-TILE = 256
+TILE = 768
+WEIGHT_ROWS = 512
 MESH = pl.DeviceIdType.MESH
 NT = (((1,), (1,)), ((), ()))
 NN = (((1,), (0,)), ((), ()))
-ITEMS = [(dx, flip, b) for dx, flip in ((0, 0), (0, 1), (-1, 0), (1, 0), (-1, 1), (1, 1), (2, 0), (2, 1)) for b in (0, 1)]
-
-
-def layer_kernel(dims, x_in, wq_in, wkv_in, wo_in, out, xs, wq, wkv, q_s, kv, m_s, l_s, acc_s, s_s, wo, o_s, ob, y_s,
-                 load_sem, x_send, x_recv, kv_send, kv_recv, wo_load, wo_send, wo_recv, ob_send, ob_recv, y_send, y_recv, y_store):
+SUBS = 4
+SECOND_EARLY = True
+WEIGHT_EVENTS = [(3, ((1, 3), (2, 0))), (4, ((3, 0), (3, 3))), (7, ((3, 1), (3, 2)))] if SECOND_EARLY else [
+    (5, ((1, 2), (2, 1))), (7, ((1, 3), (2, 0))), (9, ((3, 0), (3, 3))), (12, ((3, 1), (3, 2)))]
+ITEMS = [(dx, flip, f) for group in ([(0, 0)], [(0, 1)], [(-1, 0), (1, 0)], [(-1, 1), (1, 1)], [(2, 0)], [(2, 1)]) for f in (0, 1) for dx, flip in group]
+
+
+def layer_kernel(dims, x_in, wq_in, wk_in, wv_in, wo_in, out, raw_q, raw_k, raw_v, xs, wq, wkv, q_s, kv, m_s, l_s, acc_s, s_s, wo, o_s, ob, via, total_s, y_s,
+                 load_sem, raw_sem, x_send, x_recv, kv_send, kv_recv, wo_load, wo_send, wo_recv, ob_send, ob_recv, via_recv, far_recv, y_send, y_recv, y_store):
     sp_size, tp_size, kv_loc, group, head_dim = dims
     chips = sp_size // 2
     rows, half = 2 * xs.shape[2], xs.shape[2]
@@ -38,23 +43,47 @@
     up, down, far = (lax.rem(my_tp + d, tp_size) for d in (1, tp_size - 1, 2))
     tps = (my_tp, down, up, far)
 
+    barrier = pltpu.get_barrier_semaphore()
+    peers = [{"sp": partner}, {"sp": right}, {"sp": left}, {"tp": up}, {"tp": down}]
+    for peer in peers:
+        pl.semaphore_signal(barrier, inc=1, device_id=peer, device_id_type=MESH)
     loads = [pltpu.make_async_copy(x_in.at[pl.ds(h * half, half)], xs.at[0, h], load_sem.at[h]) for h in (0, 1)]
-    loads += [pltpu.make_async_copy(wq_in, wq, load_sem.at[2]), pltpu.make_async_copy(wkv_in, wkv, load_sem.at[3])]
     for c in loads:
         c.start()
+    step_rows = raw_q.shape[1]
+    w_chunks = xs.shape[3] // step_rows
+    raw = ((wq_in, raw_q, wq, 0), (wk_in, raw_k, wkv, 0), (wv_in, raw_v, wkv, width))
+
+    def raw_load(n, k):
+        return pltpu.make_async_copy(raw[k][0].at[pl.ds(pl.multiple_of(n * step_rows, step_rows), step_rows)], raw[k][1].at[lax.rem(n, 2)], raw_sem.at[lax.rem(n, 2), k])
+
+    def flatten_weights():
+        def body(n, carry):
+            rows_n = pl.ds(pl.multiple_of(n * step_rows, step_rows), step_rows)
+            for k, (_, src, dst, lane) in enumerate(raw):
+                raw_load(n, k).wait()
+                flat = src[lax.rem(n, 2)].reshape(step_rows, src.shape[2] * src.shape[3])
+                dst[rows_n, lane:lane + flat.shape[1]] = flat
+
+                @pl.when(n + 2 < w_chunks)
+                def _():
+                    raw_load(n + 2, k).start()
+            return carry
+
+        lax.fori_loop(0, w_chunks, body, 0)
+
+    for n in (0, 1):
+        for k in range(3):
+            raw_load(n, k).start()
     w_rows, w_cols = wo.shape[3], wo.shape[4]
 
     def columns(quarter):
         return pl.ds(pl.multiple_of((core * chips + quarter) * w_cols, w_cols), w_cols)
 
     wo_loads = [pltpu.make_async_copy(wo_in.at[pl.ds(h * w_rows, w_rows), columns(lax.rem(chip + d, chips))],
-                                      wo.at[my_tp, lax.rem(chip + d, chips), h], wo_load.at[d, h]) for d in range(chips) for h in (0, 1)]
+                                      wo.at[my_tp, lax.rem(chip + d, chips), h], wo_load.at[d, h]) for d in range(chips) for h in range(SUBS)]
     for c in wo_loads:
         c.start()
-    barrier = pltpu.get_barrier_semaphore()
-    peers = [{"sp": partner}, {"sp": right}, {"sp": left}, {"tp": up}, {"tp": down}, {"tp": far}]
-    for peer in peers:
-        pl.semaphore_signal(barrier, inc=1, device_id=peer, device_id_type=MESH)
     pl.semaphore_wait(barrier, len(peers))
 
     def x_piece(src, h, dst, peer, slot):
@@ -111,17 +140,24 @@
             device_id={"sp": partner}, device_id_type=MESH).wait_recv()
 
     to_up, to_down, to_right, to_left = {"tp": up}, {"tp": down}, {"sp": right}, {"sp": left}
-    wo_first = [wo_copy(0, 0, 0, to_up), wo_copy(0, 0, 1, to_down)]
-    wo_second = [wo_copy(0, 0, 1, to_up), wo_copy(0, 0, 0, to_down)]
-    wo_third = [wo_copy(1, 0, 0, to_up), wo_copy(2, 0, 1, to_down)]
-    wo_side = {(o, h): [wo_copy(o, 0, h, to_right), wo_copy(o, 0, h, to_left)] for o in (1, 2, 3) for h in (0, 1)}
-    wo_relay = {o: [wo_copy(o, -1, 0, to_right), wo_copy(o, 1, 1, to_left)] for o in (1, 2, 3)}
-
-    def relay(o):
-        wo_wait(o, -1, 0)
-        wo_relay[o][0].start()
-        wo_wait(o, 1, 1)
-        wo_relay[o][1].start()
+    def both_ways(pairs):
+        return [c for h in pairs for c in (wo_copy(0, 0, h, to_up), wo_copy(0, 0, SUBS - 1 - h, to_down))]
+
+    wo_first = both_ways((0, 1))
+    wo_second = both_ways((2, 3))
+    wo_third = [c for h in (0, 1) for c in (wo_copy(1, 0, h, to_up), wo_copy(2, 0, SUBS - 1 - h, to_down))]
+    wo_side = {(o, h): [wo_copy(o, 0, h, to_right), wo_copy(o, 0, h, to_left)] for o in (1, 2, 3) for h in range(SUBS)}
+    wo_relay = {(o, h): wo_copy(o, -1 if h < SUBS // 2 else 1, h, to_right if h < SUBS // 2 else to_left)
+                for o, subs in ((1, (0, 1)), (2, (3, 2)), (3, (0, 3, 1, 2))) for h in subs}
+    wo_last = [c for h in (0, 1) for c in (wo_copy(0, 2, SUBS // 2 + h, to_up), wo_copy(0, 2, h, to_down))]
+
+    def spread(o, h):
+        wo_wait(o, 0, h)
+        start(wo_side[o, h])
+
+    def relay(o, h):
+        wo_wait(o, -1 if h < SUBS // 2 else 1, h)
+        wo_relay[o, h].start()
 
     def project(step):
         x_rows = xs[step].reshape(rows, xs.shape[3])
@@ -142,49 +178,50 @@
 
     loads[0].wait()
     loads[1].wait()
-    for c in wo_loads[:2]:
+    for c in wo_loads[:SUBS]:
         c.wait()
     start(wo_first)
     start(x_sends[:4])
+    if SECOND_EARLY:
+        start(wo_second[:2])
     m_s[...] = jnp.full(m_s.shape, NEG_BIG, jnp.float32)
     l_s[...] = jnp.zeros_like(l_s)
     acc_s[...] = jnp.zeros_like(acc_s)
-    loads[2].wait()
-    loads[3].wait()
+    flatten_weights()
     def steps(step, carry):
         @pl.when(step == 1)
         def _():
             start(own_kv[0])
-            for o, h in ((1, 0), (2, 1)):
-                wo_wait(o, 0, h)
-                start(wo_side[o, h])
+            for o, h in ((1, 0), (2, 3), (1, 1), (2, 2)):
+                spread(o, h)
             x_sends[0].wait_recv()
             x_sends[4].start()
             x_sends[1].wait_recv()
             x_sends[5].start()
-            start(wo_second)
+            start(wo_second[2 if SECOND_EARLY else 0:])
             start(wo_third)
             pass_on(left_kv, left, (0,))
             pass_on(right_kv, right, (0,))
+            for c in wo_loads[SUBS:]:
+                c.wait()
 
         @pl.when(step == 2)
         def _():
+            for o, h in ((1, 0), (2, 3), (1, 1), (2, 2)):
+                relay(o, h)
             x_sends[2].wait_recv()
             x_sends[3].wait_recv()
-            pass_on(opp_kv, opp, (0,))
-            wo_wait(1, -1, 0)
-            wo_relay[1][0].start()
-            wo_wait(2, 1, 1)
-            wo_relay[2][1].start()
 
         @pl.when(step == 3)
         def _():
             start(own_kv[1])
             start(own_kv[2])
+            pass_on(opp_kv, opp, (0,))
+            if SECOND_EARLY:
+                spread(1, 2)
+                spread(2, 1)
             x_sends[4].wait_recv()
             x_sends[5].wait_recv()
-            pass_on(left_kv, left, (1, 2))
-            pass_on(right_kv, right, (1, 2))
 
         for n in range(4):
             @pl.when(step == n)
@@ -224,39 +261,63 @@
             l_s[a, g, t] = l_s[a, g, t] * alpha + jnp.sum(p, axis=0, keepdims=True)
             acc_s[a, g, t] = acc_s[a, g, t] * alpha + lax.dot_general(v_t[g], p.astype(jnp.bfloat16), NN, preferred_element_type=jnp.float32)
 
-    def wait_all(src):
-        for o in range(4):
+    def wait_for(src, orders):
+        for o in orders:
             kv_wait(src, o)
 
-    def before(i):
-        @pl.when(i == 2)
-        def _():
-            wait_all(partner)
-            pass_on(opp_kv, opp, (1, 2))
-
-        @pl.when(i == 4)
+    def before(i, past, done):
+        near = (0, 1, 2)
+
+        @pl.when((past < 3) & (done >= 3))
         def _():
             pass_on(left_kv, left, (3,))
             pass_on(right_kv, right, (3,))
 
+        for threshold, pieces in WEIGHT_EVENTS:
+            @pl.when((past < threshold) & (done >= threshold))
+            def _():
+                for o, h in pieces:
+                    if o == 3:
+                        wo_wait(o, 0, h)
+                    else:
+                        spread(o, h)
+                if pieces[0][0] == 3:
+                    first, last = (wo_side[piece] for piece in pieces)
+                    start([first[0], last[1], last[0], first[1]])
+
+        @pl.when(i == 0)
+        def _():
+            pass_on(left_kv, left, (1, 2))
+            pass_on(right_kv, right, (1, 2))
+            start(wo_last)
+
+        @pl.when(i == 2)
+        def _():
+            wait_for(partner, near)
+
+        @pl.when(i == 3)
+        def _():
+            wait_for(partner, (3,))
+
         @pl.when(i == 8)
         def _():
-            wait_all(rank(-1, 1))
-            wait_all(rank(1, 1))
+            wait_for(rank(-1, 1), near)
+            wait_for(rank(1, 1), near)
+            pass_on(opp_kv, opp, (1, 2))
+
+        @pl.when(i == 10)
+        def _():
+            wait_for(rank(-1, 1), (3,))
+            wait_for(rank(1, 1), (3,))
             pass_on(opp_kv, opp, (3,))
-            for o, h in ((1, 1), (2, 0)):
-                wo_wait(o, 0, h)
-                start(wo_side[o, h])
-
-        @pl.when(i == 12)
-        def _():
-            for h in (0, 1):
-                wo_wait(3, 0, h)
-                start(wo_side[3, h])
 
         @pl.when(i == 14)
         def _():
-            wait_all(rank(2, 1))
+            wait_for(rank(2, 1), near)
+
+        @pl.when(i == 15)
+        def _():
+            wait_for(rank(2, 1), (3,))
 
     def pick(i, field):
         out = 0
@@ -268,14 +329,19 @@
     q_ids = (me, 2 * sp_size - 1 - me)
 
     def item(i, carry):
-        before(i)
-        dx, flip, b = pick(i, 0), pick(i, 1), pick(i, 2)
+        past, done = carry
+        before(i, past, done)
+        past = done
+        dx, flip, f = pick(i, 0), pick(i, 1), pick(i, 2)
+        own_b = my_tp // 2
+        b = own_b + f - 2 * own_b * f
         src = 2 * lax.rem(chip + dx + chips, chips) + core + flip - 2 * core * flip
         k_id = b * (2 * sp_size - 1) + (1 - 2 * b) * src
         for a in range(2):
             gap = q_ids[a] - k_id
             needed = (gap >= 0) & (gap * chunk - chunk + 1 < WINDOW)
             masked = (gap == 0) | (gap * chunk + chunk - 1 >= WINDOW)
+            done = done + needed.astype(jnp.int32)
 
             @pl.when(needed & masked)
             def _():
@@ -285,9 +351,9 @@
             def _():
                 update(a, src, b, gap, False)
 
-        return carry
-
-    lax.fori_loop(0, len(ITEMS), item, 0)
+        return past, done
+
+    lax.fori_loop(0, len(ITEMS), item, (0, 0))
 
     for a in range(2):
         for g in range(kv_loc):
@@ -302,34 +368,46 @@
 
     ob_sends = []
 
-    def ob_copy(src, o, peer):
+    def ob_copy(src, dst, recv, peer):
         copy = pltpu.make_async_remote_copy(
-            src_ref=src, dst_ref=ob.at[tps[o], core], send_sem=ob_send.at[len(ob_sends)], recv_sem=ob_recv.at[tps[o], core],
-            device_id=peer, device_id_type=MESH)
+            src_ref=src, dst_ref=dst, send_sem=ob_send.at[len(ob_sends)], recv_sem=recv, device_id=peer, device_id_type=MESH)
         ob_sends.append(copy)
         return copy
 
+    def ob_wait(ref, recv):
+        pltpu.make_async_remote_copy(
+            src_ref=ref, dst_ref=ref, send_sem=ob_send.at[0], recv_sem=recv, device_id={"sp": partner}, device_id_type=MESH).wait_recv()
+
+    def part(h):
+        return pl.ds(h * half, half)
+
     ob[my_tp, core] = o_s[my_tp]
-    start([ob_copy(o_s.at[tps[o]], 0, {"tp": tps[o]}) for o in (3, 1, 2)])
-    start([ob_copy(ob.at[my_tp, core], 0, {"sp": partner})])
-
-    def ob_wait(o, c):
-        at = (tps[o], c)
-        pltpu.make_async_remote_copy(
-            src_ref=ob.at[at], dst_ref=ob.at[at], send_sem=ob_send.at[0], recv_sem=ob_recv.at[at],
-            device_id={"sp": partner}, device_id_type=MESH).wait_recv()
-
-    wo_wait(2, -1, 0)
-    wo_relay[2][0].start()
-    wo_wait(1, 1, 1)
-    wo_relay[1][1].start()
-    for o in (1, 2, 3):
-        ob_wait(o, core)
-        start([ob_copy(ob.at[tps[o], core], o, {"sp": partner})])
-    for o in range(4):
-        ob_wait(o, 1 - core)
-    for c in wo_loads[2:]:
-        c.wait()
+    start([ob_copy(o_s.at[far, part(0)], via.at[0], via_recv.at[0], to_up), ob_copy(o_s.at[far, part(1)], via.at[1], via_recv.at[1], to_down)])
+    start([ob_copy(o_s.at[up], ob.at[my_tp, core], ob_recv.at[my_tp, 0], to_up), ob_copy(o_s.at[down], ob.at[my_tp, core], ob_recv.at[my_tp, 0], to_down)])
+    start([ob_copy(ob.at[my_tp, core], ob.at[my_tp, core], ob_recv.at[my_tp, 1], {"sp": partner})])
+    def share(source, quarter):
+        return jnp.dot(ob[source].reshape(2 * rows, SUBS * w_rows), wo[source, quarter].reshape(SUBS * w_rows, w_cols), preferred_element_type=jnp.float32)
+
+    def quarter_of(n):
+        return lax.rem(chip + jnp.where(n == 1, chips - 1, jnp.where(n == 2, 1, jnp.where(n == 3, 2, 0))), chips)
+
+    def gather_own(n, carry):
+        total_s[n] = share(my_tp, quarter_of(n))
+        return carry
+
+    for h, source, peer in ((0, down, to_up), (1, up, to_down)):
+        ob_wait(via.at[h], via_recv.at[h])
+        start([ob_copy(via.at[h], ob.at[source, core, part(h)], far_recv.at[h], peer)])
+    for h in (0, 3, 1, 2):
+        relay(3, h)
+    ob_wait(ob.at[my_tp, 1 - core], ob_recv.at[my_tp, 1])
+    lax.fori_loop(0, chips, gather_own, 0)
+    for source in (down, up):
+        ob_wait(ob.at[source, core], ob_recv.at[source, 0])
+        start([ob_copy(ob.at[source, core], ob.at[source, core], ob_recv.at[source, 1], {"sp": partner})])
+    far_share = ob_copy(ob.at[far, core], ob.at[far, core], ob_recv.at[far, 1], {"sp": partner})
+    for source in (down, up):
+        ob_wait(ob.at[source, 1 - core], ob_recv.at[source, 1])
 
     def y_remote(n, quarter):
         return pltpu.make_async_remote_copy(
@@ -339,40 +417,39 @@
     def y_local(n, quarter):
         return pltpu.make_async_copy(y_s.at[n, core], out.at[:, columns(quarter)], y_store.at[n])
 
-    def quarter_of(n):
-        return lax.rem(chip + jnp.where(n == 1, chips - 1, jnp.where(n == 2, 1, jnp.where(n == 3, 2, 0))), chips)
+    def gather_near(n, carry):
+        @pl.when(n == 1)
+        def _():
+            for h in (0, 1):
+                ob_wait(ob.at[far, core, part(h)], far_recv.at[h])
+            far_share.start()
+            for o, h in ((1, 2), (1, 3), (2, 0), (2, 1), (2, 2), (2, 3), (3, 2), (3, 3)):
+                wo_wait(o, -1, h)
+
+        @pl.when(n == 2)
+        def _():
+            for o, h in ((1, 0), (1, 1), (1, 2), (1, 3), (2, 0), (2, 1), (3, 0), (3, 1)):
+                wo_wait(o, 1, h)
+
+        @pl.when(n == 3)
+        def _():
+            for o in (1, 2, 3):
+                for h in range(SUBS):
+                    wo_wait(o, 2, h)
+
+        quarter = quarter_of(n)
+        total_s[n] = total_s[n] + share(down, quarter) + share(up, quarter)
+        return carry
 
     def finish(n, carry):
-        @pl.when(n == 1)
-        def _():
-            relay(3)
-            wo_wait(1, -1, 1)
-            wo_wait(2, -1, 1)
-            wo_wait(3, -1, 1)
-
-        @pl.when(n == 2)
-        def _():
-            for o in (1, 2, 3):
-                wo_wait(o, 1, 0)
-
-        @pl.when(n == 3)
-        def _():
-            for o in (1, 2, 3):
-                for h in (0, 1):
-                    wo_wait(o, 2, h)
-
         quarter = quarter_of(n)
-        for part in range(0, w_cols, TILE):
-            total = None
-            for tp in range(tp_size):
-                res = jnp.dot(ob[tp].reshape(2 * rows, 2 * w_rows), wo[tp, quarter, :, :, part:part + TILE].reshape(2 * w_rows, TILE),
-                              preferred_element_type=jnp.float32)
-                total = res if total is None else total + res
-            y_s[n, :, :, part:part + TILE] = total.astype(jnp.bfloat16).reshape(2, rows, TILE)
+        y_s[n] = (total_s[n] + share(far, quarter)).astype(jnp.bfloat16).reshape(2, rows, w_cols)
         y_remote(n, quarter).start()
         y_local(n, quarter).start()
         return carry
 
+    lax.fori_loop(0, chips, gather_near, 0)
+    ob_wait(ob.at[far, 1 - core], ob_recv.at[far, 1])
     lax.fori_loop(0, chips, finish, 0)
     for n in range(chips):
         y_remote(n, quarter_of(n)).wait()
@@ -381,7 +458,7 @@
         c.wait_send()
 
 
-def layer(sp_size, tp_size, heads, x_part, w_q, w_kv, w_o):
+def layer(sp_size, tp_size, heads, x_part, w_q, w_k, w_v, w_o):
     kv_loc, group, head_dim = heads
     rows, d_model = x_part.shape
     chunk = 2 * rows
@@ -395,27 +472,32 @@
         functools.partial(layer_kernel, (sp_size, tp_size) + heads),
         name="layer",
         out_shape=jax.ShapeDtypeStruct(x_part.shape, bf16),
-        in_specs=[pl.BlockSpec(memory_space=pl.ANY)] * 4,
+        in_specs=[pl.BlockSpec(memory_space=pl.ANY)] * 5,
         out_specs=pl.BlockSpec(memory_space=pl.ANY),
         scratch_shapes=[
+            pltpu.VMEM((2, WEIGHT_ROWS) + w_q.shape[1:], bf16),
+            pltpu.VMEM((2, WEIGHT_ROWS) + w_k.shape[1:], bf16),
+            pltpu.VMEM((2, WEIGHT_ROWS) + w_v.shape[1:], bf16),
             pltpu.VMEM((4, 2, rows // 2, d_model), bf16),
-            pltpu.VMEM(w_q.shape, bf16),
-            pltpu.VMEM(w_kv.shape, bf16),
+            pltpu.VMEM((d_model, group * width), bf16),
+            pltpu.VMEM((d_model, 2 * width), bf16),
             pltpu.VMEM((2, kv_loc, group * chunk, head_dim), bf16),
             pltpu.VMEM((sp_size, tp_size, rows, 2 * width), bf16),
             pltpu.VMEM((2, kv_loc, tiles, 1, TILE), f32),
             pltpu.VMEM((2, kv_loc, tiles, 1, TILE), f32),
             pltpu.VMEM((2, kv_loc, tiles, head_dim, TILE), f32),
             pltpu.VMEM((2, chunk, TILE), f32),
-            pltpu.VMEM((tp_size, chips, 2, w_o.shape[0] // 2, quarter), bf16),
+            pltpu.VMEM((tp_size, chips, SUBS, w_o.shape[0] // SUBS, quarter), bf16),
             pltpu.VMEM((tp_size, rows, w_o.shape[0]), bf16),
             pltpu.VMEM((tp_size, 2, rows, w_o.shape[0]), bf16),
+            pltpu.VMEM((2, rows // 2, w_o.shape[0]), bf16),
+            pltpu.VMEM((chips, 2 * rows, quarter), f32),
             pltpu.VMEM((chips, 2, rows, quarter), bf16),
-            dma((4,)), dma((6,)), dma((4, 2)), dma((28,)), dma((sp_size, tp_size)),
-            dma((chips, 2)), dma((24,)), dma((tp_size, chips, 2)), dma((7,)), dma((tp_size, 2)), dma((chips,)), dma((chips,)), dma((chips,)),
+            dma((2,)), dma((2, 3)), dma((6,)), dma((4, 2)), dma((28,)), dma((sp_size, tp_size)),
+            dma((chips, SUBS)), dma((48,)), dma((tp_size, chips, SUBS)), dma((10,)), dma((tp_size, 2)), dma((2,)), dma((2,)), dma((chips,)), dma((chips,)), dma((chips,)),
         ],
         compiler_params=pltpu.CompilerParams(collective_id=1, has_side_effects=True, vmem_limit_bytes=62 << 20),
-    )(x_part, w_q, w_kv, w_o)
+    )(x_part, w_q, w_k, w_v, w_o)
 
 
 def solution(mesh):
@@ -425,9 +507,7 @@
         d_model = x_part.shape[1]
         heads_loc, head_dim = w_query.shape[1], w_query.shape[2]
         kv_loc = w_key.shape[1]
-        w_q = w_query.reshape(d_model, -1)
-        w_kv = jnp.concatenate([w_key.reshape(d_model, -1), w_value.reshape(d_model, -1)], axis=1)
         w_o = w_out.reshape(-1, d_model)
-        return layer(sp_size, tp_size, (kv_loc, heads_loc // kv_loc, head_dim), x_part, w_q, w_kv, w_o)
+        return layer(sp_size, tp_size, (kv_loc, heads_loc // kv_loc, head_dim), x_part, w_query, w_key, w_value, w_o)
 
     return jax.shard_map(local_attn, mesh=mesh, in_specs=(P(("dp", "sp", "tp"), None), P(None, "tp", None), P(None, "tp", None), P(None, "tp", None), P("tp", None, None)), out_specs=P(("dp", "sp", "tp"), None), check_vma=False)

time: 189 us -> 149 us (0.79)
  Pallas kernels: 172 us -> 146 us
  local copies, waits for them, and re-layouts: 14.4 us -> 2.7 us
  other arithmetic: 2.31 us -> 0 us
    pallas_call x1, Pallas kernels: 172 us -> 146 us  [layer(): pl.pallas_call(functools.partial(layer_kernel, (sp_size, tp_size) + heads...]
    unnamed x2 -> x1, local copies, waits for them, and re-layouts: 11.5 us -> 2.7 us
    reshape x1 -> x0, local copies, waits for them, and re-layouts: 2.89 us -> none  [local_attn(): w_value.reshape(d_model, -1)]
    concatenate x1 -> x0, other arithmetic: 2.31 us -> none  [local_attn(): jnp.concatenate([w_key.reshape(d_model, -1), w_value.reshape(d_model, -1)...]
where the time goes in v3:
time: 149 us
  Pallas kernels  146 us (98%)
  local copies, waits for them, and re-layouts  2.7 us (2%)
    pallas_call x1, Pallas kernels, layer(): pl.pallas_call(functools.partial(layer_kernel, (sp_size, tp_size) + heads...  146 us

profile of v3, /device:TPU:97, one launch (start us, length us, event | category | flops | bytes accessed | tf_op | source)
XLA Modules:
  0.0 149.0 jit_solution(11931012765623069399)
XLA Ops:
  0.0 146.3 %layer.1 = bf16[192,4096]{1,0:T(8,128)(2,1)} custom-call(bf16[192,4096]{1,0:T(8,128)(2,1)} %x_in.1, bf16[4096,8,128]{2,1,0:T(8,128)(2,1)} %wq_in.1, bf16[4096,2,128]{2,1,0:T(2,128)(2,1)} %wk_in.1, bf16[4096,2,128]{2,1,0:T(2,128)(2,1)} %wv_in.1, bf16[1024,4096]{1,0:T(8,128)(2,1)} %bitcast.1), custom_call_target="tpu_custom_call" | custom-call | tf_op jit(solution)/shard_map/layer/pallas_call | solution.py:471
  146.3 2.7 %copy.7 = bf16[192,4096]{1,0:T(8,128)(2,1)} copy(bf16[192,4096]{1,0:T(8,128)(2,1)} %layer.1) | data formatting | bytes 3145728

commit v4 on v3

--- a/solution.py
+++ b/solution.py
@@ -16,9 +16,7 @@
 NT = (((1,), (1,)), ((), ()))
 NN = (((1,), (0,)), ((), ()))
 SUBS = 4
-SECOND_EARLY = True
-WEIGHT_EVENTS = [(3, ((1, 3), (2, 0))), (4, ((3, 0), (3, 3))), (7, ((3, 1), (3, 2)))] if SECOND_EARLY else [
-    (5, ((1, 2), (2, 1))), (7, ((1, 3), (2, 0))), (9, ((3, 0), (3, 3))), (12, ((3, 1), (3, 2)))]
+WEIGHT_EVENTS = [(3, ((3, 0), (3, 3))), (5, ((3, 1), (3, 2))), (8, ((1, 3), (2, 0)))]
 ITEMS = [(dx, flip, f) for group in ([(0, 0)], [(0, 1)], [(-1, 0), (1, 0)], [(-1, 1), (1, 1)], [(2, 0)], [(2, 1)]) for f in (0, 1) for dx, flip in group]
 
 
@@ -146,10 +144,12 @@
     wo_first = both_ways((0, 1))
     wo_second = both_ways((2, 3))
     wo_third = [c for h in (0, 1) for c in (wo_copy(1, 0, h, to_up), wo_copy(2, 0, SUBS - 1 - h, to_down))]
-    wo_side = {(o, h): [wo_copy(o, 0, h, to_right), wo_copy(o, 0, h, to_left)] for o in (1, 2, 3) for h in range(SUBS)}
+    wo_side = {(o, h): [wo_copy(o, 0, h, peer) for peer, direct in ((to_right, (1, 3)), (to_left, (2, 0))) if (o, h) != direct]
+               for o in (1, 2, 3) for h in range(SUBS)}
     wo_relay = {(o, h): wo_copy(o, -1 if h < SUBS // 2 else 1, h, to_right if h < SUBS // 2 else to_left)
                 for o, subs in ((1, (0, 1)), (2, (3, 2)), (3, (0, 3, 1, 2))) for h in subs}
     wo_last = [c for h in (0, 1) for c in (wo_copy(0, 2, SUBS // 2 + h, to_up), wo_copy(0, 2, h, to_down))]
+    wo_last += [wo_copy(0, -1, 3, to_up), wo_copy(0, 1, 0, to_down)]
 
     def spread(o, h):
         wo_wait(o, 0, h)
@@ -182,24 +182,25 @@
         c.wait()
     start(wo_first)
     start(x_sends[:4])
-    if SECOND_EARLY:
-        start(wo_second[:2])
+    start(wo_second[:2])
     m_s[...] = jnp.full(m_s.shape, NEG_BIG, jnp.float32)
     l_s[...] = jnp.zeros_like(l_s)
     acc_s[...] = jnp.zeros_like(acc_s)
     flatten_weights()
+    spread(1, 0)
+    spread(2, 3)
     def steps(step, carry):
         @pl.when(step == 1)
         def _():
             start(own_kv[0])
-            for o, h in ((1, 0), (2, 3), (1, 1), (2, 2)):
-                spread(o, h)
+            spread(1, 1)
+            spread(2, 2)
             x_sends[0].wait_recv()
             x_sends[4].start()
             x_sends[1].wait_recv()
             x_sends[5].start()
-            start(wo_second[2 if SECOND_EARLY else 0:])
             start(wo_third)
+            start(wo_second[2:])
             pass_on(left_kv, left, (0,))
             pass_on(right_kv, right, (0,))
             for c in wo_loads[SUBS:]:
@@ -217,9 +218,8 @@
             start(own_kv[1])
             start(own_kv[2])
             pass_on(opp_kv, opp, (0,))
-            if SECOND_EARLY:
-                spread(1, 2)
-                spread(2, 1)
+            spread(1, 2)
+            spread(2, 1)
             x_sends[4].wait_recv()
             x_sends[5].wait_recv()
 
@@ -354,6 +354,8 @@
         return past, done
 
     lax.fori_loop(0, len(ITEMS), item, (0, 0))
+    relay(3, 0)
+    relay(3, 3)
 
     for a in range(2):
         for g in range(kv_loc):
@@ -386,7 +388,13 @@
     start([ob_copy(o_s.at[up], ob.at[my_tp, core], ob_recv.at[my_tp, 0], to_up), ob_copy(o_s.at[down], ob.at[my_tp, core], ob_recv.at[my_tp, 0], to_down)])
     start([ob_copy(ob.at[my_tp, core], ob.at[my_tp, core], ob_recv.at[my_tp, 1], {"sp": partner})])
     def share(source, quarter):
-        return jnp.dot(ob[source].reshape(2 * rows, SUBS * w_rows), wo[source, quarter].reshape(SUBS * w_rows, w_cols), preferred_element_type=jnp.float32)
+        res = jnp.dot(ob[source].reshape(2 * rows, SUBS * w_rows), wo[source, quarter].reshape(SUBS * w_rows, w_cols), preferred_element_type=jnp.float32)
+        return res.reshape(2, rows, w_cols)
+
+    def add_near(n, c):
+        quarter = quarter_of(n)
+        res = [jnp.dot(ob[source, c], wo[source, quarter].reshape(SUBS * w_rows, w_cols), preferred_element_type=jnp.float32) for source in (down, up)]
+        total_s[n, c] = total_s[n, c] + res[0] + res[1]
 
     def quarter_of(n):
         return lax.rem(chip + jnp.where(n == 1, chips - 1, jnp.where(n == 2, 1, jnp.where(n == 3, 2, 0))), chips)
@@ -398,26 +406,16 @@
     for h, source, peer in ((0, down, to_up), (1, up, to_down)):
         ob_wait(via.at[h], via_recv.at[h])
         start([ob_copy(via.at[h], ob.at[source, core, part(h)], far_recv.at[h], peer)])
-    for h in (0, 3, 1, 2):
-        relay(3, h)
+    relay(3, 1)
+    relay(3, 2)
     ob_wait(ob.at[my_tp, 1 - core], ob_recv.at[my_tp, 1])
     lax.fori_loop(0, chips, gather_own, 0)
     for source in (down, up):
         ob_wait(ob.at[source, core], ob_recv.at[source, 0])
         start([ob_copy(ob.at[source, core], ob.at[source, core], ob_recv.at[source, 1], {"sp": partner})])
     far_share = ob_copy(ob.at[far, core], ob.at[far, core], ob_recv.at[far, 1], {"sp": partner})
-    for source in (down, up):
-        ob_wait(ob.at[source, 1 - core], ob_recv.at[source, 1])
-
-    def y_remote(n, quarter):
-        return pltpu.make_async_remote_copy(
-            src_ref=y_s.at[n, 1 - core], dst_ref=out.at[:, columns(quarter)], send_sem=y_send.at[n], recv_sem=y_recv.at[n],
-            device_id={"sp": partner}, device_id_type=MESH)
-
-    def y_local(n, quarter):
-        return pltpu.make_async_copy(y_s.at[n, core], out.at[:, columns(quarter)], y_store.at[n])
-
-    def gather_near(n, carry):
+
+    def near_rows(n, carry):
         @pl.when(n == 1)
         def _():
             for h in (0, 1):
@@ -431,25 +429,36 @@
             for o, h in ((1, 0), (1, 1), (1, 2), (1, 3), (2, 0), (2, 1), (3, 0), (3, 1)):
                 wo_wait(o, 1, h)
 
-        @pl.when(n == 3)
+        add_near(n, core)
+        return carry
+
+    lax.fori_loop(0, chips - 1, near_rows, 0)
+    for source in (down, up, far):
+        ob_wait(ob.at[source, 1 - core], ob_recv.at[source, 1])
+
+    def y_remote(n, quarter):
+        return pltpu.make_async_remote_copy(
+            src_ref=y_s.at[n, 1 - core], dst_ref=out.at[:, columns(quarter)], send_sem=y_send.at[n], recv_sem=y_recv.at[n],
+            device_id={"sp": partner}, device_id_type=MESH)
+
+    def y_local(n, quarter):
+        return pltpu.make_async_copy(y_s.at[n, core], out.at[:, columns(quarter)], y_store.at[n])
+
+    def finish(n, carry):
+        @pl.when(n == chips - 1)
         def _():
             for o in (1, 2, 3):
                 for h in range(SUBS):
                     wo_wait(o, 2, h)
-
+            add_near(n, core)
+
+        add_near(n, 1 - core)
         quarter = quarter_of(n)
-        total_s[n] = total_s[n] + share(down, quarter) + share(up, quarter)
-        return carry
-
-    def finish(n, carry):
-        quarter = quarter_of(n)
-        y_s[n] = (total_s[n] + share(far, quarter)).astype(jnp.bfloat16).reshape(2, rows, w_cols)
+        y_s[n] = (total_s[n] + share(far, quarter)).astype(jnp.bfloat16)
         y_remote(n, quarter).start()
         y_local(n, quarter).start()
         return carry
 
-    lax.fori_loop(0, chips, gather_near, 0)
-    ob_wait(ob.at[far, 1 - core], ob_recv.at[far, 1])
     lax.fori_loop(0, chips, finish, 0)
     for n in range(chips):
         y_remote(n, quarter_of(n)).wait()
@@ -491,7 +500,7 @@
             pltpu.VMEM((tp_size, rows, w_o.shape[0]), bf16),
             pltpu.VMEM((tp_size, 2, rows, w_o.shape[0]), bf16),
             pltpu.VMEM((2, rows // 2, w_o.shape[0]), bf16),
-            pltpu.VMEM((chips, 2 * rows, quarter), f32),
+            pltpu.VMEM((chips, 2, rows, quarter), f32),
             pltpu.VMEM((chips, 2, rows, quarter), bf16),
             dma((2,)), dma((2, 3)), dma((6,)), dma((4, 2)), dma((28,)), dma((sp_size, tp_size)),
             dma((chips, SUBS)), dma((48,)), dma((tp_size, chips, SUBS)), dma((10,)), dma((tp_size, 2)), dma((2,)), dma((2,)), dma((chips,)), dma((chips,)), dma((chips,)),

time: 149 us -> 142 us (0.953)
  Pallas kernels: 146 us -> 139 us
    pallas_call x1, Pallas kernels: 146 us -> 139 us  [layer(): pl.pallas_call(functools.partial(layer_kernel, (sp_size, tp_size) + heads...]
where the time goes in v4:
time: 142 us
  Pallas kernels  139 us (98%)
  local copies, waits for them, and re-layouts  2.7 us (2%)
    pallas_call x1, Pallas kernels, layer(): pl.pallas_call(functools.partial(layer_kernel, (sp_size, tp_size) + heads...  139 us

profile of v4, /device:TPU:97, one launch (start us, length us, event | category | flops | bytes accessed | tf_op | source)
XLA Modules:
  0.0 141.6 jit_solution(12656655247825386211)
XLA Ops:
  0.0 138.9 %layer.1 = bf16[192,4096]{1,0:T(8,128)(2,1)} custom-call(bf16[192,4096]{1,0:T(8,128)(2,1)} %x_in.1, bf16[4096,8,128]{2,1,0:T(8,128)(2,1)} %wq_in.1, bf16[4096,2,128]{2,1,0:T(2,128)(2,1)} %wk_in.1, bf16[4096,2,128]{2,1,0:T(2,128)(2,1)} %wv_in.1, bf16[1024,4096]{1,0:T(8,128)(2,1)} %bitcast.1), custom_call_target="tpu_custom_call" | custom-call | tf_op jit(solution)/shard_map/layer/pallas_call | solution.py:480
  138.9 2.7 %copy.7 = bf16[192,4096]{1,0:T(8,128)(2,1)} copy(bf16[192,4096]{1,0:T(8,128)(2,1)} %layer.1) | data formatting | bytes 3145728
